TPU v7x, 32 devices: a 4x4x1 block of a 4x4x8 slice. The times are simulated.
32 devices in a mesh: rep: 1 (over z), dp: 32 (over x, y, core).
Axes of the slice: x: 4, y: 4, z: 1, core: 2. Of those that a mesh axis runs over, the one named last changes fastest.
The devices are a block of a 4x4x8 slice.
Arguments:
- x: bfloat16 [32, 2048, 896], P(('rep', 'dp'))
- dy: bfloat16 [32, 2048, 896], P(('rep', 'dp'))
- w_gate: bfloat16 [2, 896, 2304], P(None, 'dp')
- w_up: bfloat16 [2, 896, 2304], P(None, 'dp')
- w_down: bfloat16 [2, 2304, 896], P(None, 'dp')
Outputs:
- output 1: bfloat16 [32, 2048, 896], P(('rep', 'dp'))
- output 2: bfloat16 [2, 896, 2304], P('rep', 'dp')
- output 3: bfloat16 [2, 896, 2304], P('rep', 'dp')
- output 4: bfloat16 [2, 2304, 896], P('rep', 'dp')
All inputs are finite; a program needn't handle non-finite values.
Results may differ from a plain program's by a relative error of at most 0.018.
Values are sent between devices in bfloat16 or wider.
A program may use at most 768 MiB of HBM per device.

v0:
```python
import jax
import jax.numpy as jnp
from jax import lax

NAMES = ("w_gate", "w_up", "w_down")


def matmul(a, w):
    return jnp.dot(a, w, preferred_element_type=jnp.float32).astype(jnp.bfloat16)


def normed(h):
    wide = h.astype(jnp.float32)
    scale = lax.rsqrt(jnp.mean(wide**2, -1, keepdims=True) + 1e-6)
    return (wide * scale).astype(jnp.bfloat16)


def layer(h, w):
    a = normed(h)
    gate = jnp.dot(a, w["w_gate"], preferred_element_type=jnp.float32)
    up = jnp.dot(a, w["w_up"], preferred_element_type=jnp.float32)
    return h + matmul((jax.nn.silu(gate) * up).astype(jnp.bfloat16), w["w_down"])


def stack(weights, h):
    for number in range(weights["w_gate"].shape[0]):
        h = layer(h, {name: w[number] for name, w in weights.items()})
    return h


def solution(mesh):
    groups = mesh.shape["rep"]

    def step(x, dy, *weights):
        shape = x.shape
        x, dy = (t.reshape(groups, -1, *t.shape[1:]) for t in (x, dy))

        def of_a_group(x, dy):
            _, back = jax.vjp(stack, dict(zip(NAMES, weights, strict=True)), x)
            by_weights, by_x = back(dy)
            return (by_x, *(by_weights[name] for name in NAMES))

        by_x, *by_weights = jax.vmap(of_a_group)(x, dy)
        return (by_x.reshape(shape), *(t.reshape(-1, *t.shape[2:]) for t in by_weights))

    return step
```

profile of v0, /device:TPU:97, one launch (start us, length us, event | category | flops | bytes accessed | tf_op | source)
XLA Modules:
  0.0 970.0 jit_solution(5769970901117607412)
XLA Ops:
  31.6 30.0 %all-gather.30.cloned.1.call-done = bf16[1,896,2304]{2,0,1:T(2,128)(2,1)} async-done(((bf16[1,28,2304]{2,0,1:T(2,128)(2,1)}), bf16[1,896,2304]{2,0,1:T(2,128)(2,1)}) %all-gather.30.cloned.1.call-update) | async-done | bytes 4128784 | tf_op jit(solution)/vmap(jvp())/squeeze | solution.py:27
  61.6 17.9 %fusion.56 = f32[2048,2304]{1,0:T(8,128)} fusion(bf16[1,2048,896]{1,2,0:T(8,128)(2,1)} %copy.17, f32[2048]{0:T(1024)S(1)} %bitcast.245, bf16[1,896,2304]{2,0,1:T(2,128)(2,1)} %all-gather.30.cloned.1.call-done), kind=kOutput, calls=%fused_computation.73 | convolution fusion | flops 8461221888 | bytes 26681344 | tf_op jit(solution)/vmap(jvp())/dot_general | solution.py:20
  79.4 31.4 %all-gather.32.cloned.1.call-done = bf16[1,896,2304]{2,0,1:T(2,128)(2,1)} async-done(((bf16[1,28,2304]{2,0,1:T(2,128)(2,1)}), bf16[1,896,2304]{2,0,1:T(2,128)(2,1)}) %all-gather.32.cloned.1.call-update) | async-done | bytes 4128784 | tf_op jit(solution)/vmap(jvp())/squeeze | solution.py:27
  110.9 18.0 %fusion.52 = f32[2048,2304]{1,0:T(8,128)} fusion(bf16[1,2048,896]{1,2,0:T(8,128)(2,1)} %copy.17, f32[2048]{0:T(1024)S(1)} %bitcast.246, bf16[1,896,2304]{2,0,1:T(2,128)(2,1)} %all-gather.32.cloned.1.call-done), kind=kOutput, calls=%fused_computation.69 | convolution fusion | flops 8461221888 | bytes 26681344 | tf_op jit(solution)/vmap(jvp())/dot_general | solution.py:21
  153.2 14.9 %fusion.41 = (f32[2048]{0:T(1024)S(1)}, bf16[1,2048,896]{1,2,0:T(8,128)(2,1)}) fusion(bf16[1,2048,896]{1,2,0:T(8,128)(2,1)} %copy.17, bf16[2048,2304]{1,0:T(8,128)(2,1)} %fusion.30, bf16[1,2304,896]{2,1,0:T(8,128)(2,1)} %all-gather.34.cloned.1.call-done), kind=kOutput, calls=%fused_computation.58 | convolution fusion | flops 8464889856 | bytes 20914176 | tf_op jit(solution)/vmap(jvp())/dot_general | solution.py:9
  168.7 26.5 %all-gather.38.cloned.1.call-done = bf16[1,2304,896]{2,1,0:T(8,128)(2,1)} async-done(((bf16[1,72,896]{2,1,0:T(8,128)(2,1)}), bf16[1,2304,896]{2,1,0:T(8,128)(2,1)}) %all-gather.38.cloned.1.call-update) | async-done | bytes 4128784 | tf_op jit(solution)/vmap(jvp())/squeeze | solution.py:27
  195.2 15.0 %fusion.28 = bf16[1,2048,2304]{2,1,0:T(8,128)(2,1)} fusion(bf16[1,2304,896]{2,1,0:T(8,128)(2,1)} %all-gather.38.cloned.1.call-done, bf16[1,2048,896]{2,1,0:T(8,128)(2,1)} %param), kind=kOutput, calls=%fused_computation.44 | convolution fusion | flops 8460435456 | bytes 17235968 | tf_op jit(solution)/vmap(transpose(jvp()))/dot_general | solution.py:9
  210.2 34.1 %all-gather.36.cloned.1.call-done = bf16[1,896,2304]{2,0,1:T(2,128)(2,1)} async-done(((bf16[1,28,2304]{2,0,1:T(2,128)(2,1)}), bf16[1,896,2304]{2,0,1:T(2,128)(2,1)}) %all-gather.36.cloned.1.call-update) | async-done | bytes 4128784 | tf_op jit(solution)/vmap(jvp())/squeeze | solution.py:27
  244.2 18.3 %fusion.49 = f32[2048,2304]{1,0:T(8,128)} fusion(bf16[1,2048,896]{1,2,0:T(8,128)(2,1)} %get-tuple-element.31, f32[2048]{0:T(1024)S(1)} %bitcast.250, bf16[1,896,2304]{2,0,1:T(2,128)(2,1)} %all-gather.36.cloned.1.call-done), kind=kOutput, calls=%fused_computation.66 | convolution fusion | flops 8461221888 | bytes 26681344 | tf_op jit(solution)/vmap(jvp())/dot_general | solution.py:20
  262.5 17.5 %fusion.24 = f32[2304,896]{0,1:T(8,128)} fusion(bf16[1,2048,2304]{2,1,0:T(8,128)(2,1)} %fusion.28, f32[2048,2304]{1,0:T(8,128)} %fusion.49, bf16[1,2048,896]{1,2,0:T(8,128)(2,1)S(1)} %copy-done.8, f32[2048]{0:T(1024)S(1)} %bitcast.251), kind=kOutput, calls=%fused_computation.32 | convolution fusion | flops 8489533440 | bytes 40247296 | tf_op jit(solution)/vmap(transpose(jvp()))/dot_general | solution.py:21
  280.0 91.6 %fusion.2 = f32[2304,32]{0,1:T(8,128)S(1)} fusion(f32[2304,896]{0,1:T(8,128)} %fusion.24), kind=kCustom, calls=%all-reduce-scatter.2 | all-reduce-scatter fusion | flops 2359297 | bytes 8552448
  393.1 22.2 %fusion.8 = bf16[2048,2304]{1,0:T(8,128)(2,1)} fusion(f32[2048,2304]{1,0:T(8,128)} %fusion.49, f32[2048,2304]{1,0:T(8,128)S(1)} %fusion.44, bf16[1,2048,2304]{2,1,0:T(8,128)(2,1)} %fusion.28), kind=kLoop, calls=%fused_computation.10 | loop fusion | flops 56623104 | bytes 56623104
  415.3 16.1 %fusion.47 = bf16[2048,896]{0,1:T(8,128)(2,1)} fusion(bf16[2048,2304]{1,0:T(8,128)(2,1)} %fusion.8, bf16[1,896,2304]{2,0,1:T(2,128)(2,1)} %all-gather.36.cloned.1.call-done), kind=kOutput, calls=%fused_computation.64 | convolution fusion | flops 8455716864 | bytes 17235968 | tf_op jit(solution)/vmap(transpose(jvp()))/dot_general | solution.py:20
  431.4 19.8 %fusion.43 = (f32[2048]{0:T(1024)S(1)}, bf16[2048,896]{0,1:T(8,128)(2,1)S(1)}) fusion(bf16[1,2048,896]{1,2,0:T(8,128)(2,1)} %get-tuple-element.31, bf16[2048,896]{0,1:T(8,128)(2,1)} %fusion.47, bf16[1,896,2304]{2,0,1:T(2,128)(2,1)} %all-gather.40.cloned.1.call-done, bf16[1,2048,2304]{2,1,0:T(8,128)(2,1)} %fusion.28, f32[2048,2304]{1,0:T(8,128)} %fusion.49), kind=kOutput, calls=%fused_computation.60 | convolution fusion | flops 8495036416 | bytes 43458560 | tf_op jit(solution)/vmap(transpose(jvp()))/dot_general | solution.py:21
  470.8 15.7 %fusion.29 = bf16[1,2048,2304]{2,1,0:T(8,128)(2,1)} fusion(bf16[1,2304,896]{2,1,0:T(8,128)(2,1)} %all-gather.34.cloned.1.call-done, bf16[1,2048,896]{1,2,0:T(8,128)(2,1)} %copy-done.6), kind=kOutput, calls=%fused_computation.45 | convolution fusion | flops 8460435456 | bytes 17235968 | tf_op jit(solution)/vmap(transpose(jvp()))/dot_general | solution.py:9
  486.6 17.5 %fusion.20 = f32[2304,896]{0,1:T(8,128)} fusion(bf16[1,2048,2304]{2,1,0:T(8,128)(2,1)} %fusion.29, f32[2048,2304]{1,0:T(8,128)} %fusion.56, bf16[1,2048,896]{1,2,0:T(8,128)(2,1)S(1)} %copy-done.1, f32[2048]{0:T(1024)S(1)} %bitcast.247), kind=kOutput, calls=%fused_computation.30 | convolution fusion | flops 8489533440 | bytes 40247296 | tf_op jit(solution)/vmap(transpose(jvp()))/dot_general | solution.py:21
  504.0 88.8 %fusion.3 = f32[2304,32]{0,1:T(8,128)S(1)} fusion(f32[2304,896]{0,1:T(8,128)} %fusion.20), kind=kCustom, calls=%all-reduce-scatter.3 | all-reduce-scatter fusion | flops 2359297 | bytes 8552448
  593.6 20.4 %fusion.11 = bf16[2048,2304]{1,0:T(8,128)(2,1)} fusion(f32[2048,2304]{1,0:T(8,128)} %fusion.56, f32[2048,2304]{1,0:T(8,128)} %fusion.52, bf16[1,2048,2304]{2,1,0:T(8,128)(2,1)} %fusion.29), kind=kLoop, calls=%fused_computation.13 | loop fusion | flops 56623104 | bytes 56623104
  618.1 15.1 %fusion.87 = f32[2304,896]{0,1:T(8,128)} fusion(bf16[2048,2304]{1,0:T(8,128)(2,1)} %fusion.8, bf16[1,2048,896]{1,2,0:T(8,128)(2,1)} %get-tuple-element.31, f32[2048]{0:T(1024)S(1)} %bitcast.254), kind=kOutput, calls=%fused_computation.92 | convolution fusion | flops 8461221888 | bytes 21372928 | tf_op jit(solution)/vmap(transpose(jvp()))/dot_general | solution.py:20
  644.7 20.1 %fusion.32 = f32[2304,896]{1,0:T(8,128)} fusion(f32[2048,2304]{1,0:T(8,128)} %copy-done.4, f32[2048,2304]{1,0:T(8,128)} %fusion.49, bf16[1,2048,896]{2,1,0:T(8,128)(2,1)} %param), kind=kOutput, calls=%fused_computation.48 | convolution fusion | flops 8484028416 | bytes 49676288 | tf_op jit(solution)/vmap(transpose(jvp()))/dot_general | solution.py:9
  664.8 90.0 %fusion = f32[2304,32]{0,1:T(8,128)S(1)} fusion(f32[2304,896]{0,1:T(8,128)} %fusion.87), kind=kCustom, calls=%all-reduce-scatter | all-reduce-scatter fusion | flops 2359297 | bytes 8552448
  755.0 16.5 %fusion.54 = bf16[2048,896]{0,1:T(8,128)(2,1)} fusion(bf16[2048,2304]{1,0:T(8,128)(2,1)} %fusion.11, bf16[1,896,2304]{2,0,1:T(2,128)(2,1)} %all-gather.30.cloned.1.call-done), kind=kOutput, calls=%fused_computation.71 | convolution fusion | flops 8455716864 | bytes 17235968 | tf_op jit(solution)/vmap(transpose(jvp()))/dot_general | solution.py:20
  771.5 18.3 %fusion.40 = (f32[2048]{0:T(1024)S(1)}, bf16[2048,896]{0,1:T(8,128)(2,1)}) fusion(bf16[1,2048,896]{1,2,0:T(8,128)(2,1)S(1)} %copy-done.3, bf16[2048,896]{0,1:T(8,128)(2,1)} %fusion.54, bf16[1,896,2304]{2,0,1:T(2,128)(2,1)} %all-gather.32.cloned.1.call-done, bf16[1,2048,2304]{2,1,0:T(8,128)(2,1)S(1)} %bitcast.238, f32[2048,2304]{1,0:T(8,128)} %fusion.56), kind=kOutput, calls=%fused_computation.57 | convolution fusion | flops 8495036416 | bytes 43458560 | tf_op jit(solution)/vmap(transpose(jvp()))/dot_general | solution.py:21
  789.8 101.9 %fusion.1 = f32[2304,32]{0,1:T(8,128)S(1)} fusion(f32[2304,896]{0,1:T(8,128)} %fusion.82), kind=kCustom, calls=%all-reduce-scatter.1 | all-reduce-scatter fusion | flops 2359297 | bytes 8552448
  (149 shorter events, 177.2 us)
Async XLA Ops:
  7.2 54.4 %all-gather.30.cloned.1.call-start = ((), (), s32[]{:S(2)}) async-start(), calls=%async_computation.2 | async-start | bytes 8515584 | tf_op jit(solution)/vmap(jvp())/squeeze | solution.py:27
  9.6 101.3 %all-gather.32.cloned.1.call-start = ((), (), s32[]{:S(2)}) async-start(), calls=%async_computation.3 | async-start | bytes 8515584 | tf_op jit(solution)/vmap(jvp())/squeeze | solution.py:27
  12.0 141.1 %all-gather.34.cloned.1.call-start = ((), (), s32[]{:S(2)}) async-start(), calls=%async_computation.4 | async-start | bytes 4257792 | tf_op jit(solution)/vmap(jvp())/squeeze | solution.py:27
  13.9 181.3 %all-gather.38.cloned.1.call-start = ((), (), s32[]{:S(2)}) async-start(), calls=%async_computation.6 | async-start | bytes 4257792 | tf_op jit(solution)/vmap(jvp())/squeeze | solution.py:27
  14.5 229.7 %all-gather.36.cloned.1.call-start = ((), (), s32[]{:S(2)}) async-start(), calls=%async_computation.5 | async-start | bytes 8515584 | tf_op jit(solution)/vmap(jvp())/squeeze | solution.py:27
  15.2 363.8 %all-gather.40.cloned.1.call-start = ((), (), s32[]{:S(2)}) async-start(), calls=%async_computation.7 | async-start | bytes 8515584 | tf_op jit(solution)/vmap(jvp())/squeeze | solution.py:27
  15.8 944.2 %reduce-scatter.23.cloned.1.call-start = ((), (), s32[]{:S(2)}) async-start(), calls=%async_computation.9 | async-start | bytes 8515584
  373.1 519.9 %collective-permute-start.10 = (bf16[2304,32]{0,1:T(8,128)(2,1)}, bf16[2304,32]{0,1:T(8,128)(2,1)}, u32[]{:S(2)}, u32[]{:S(2)}) collective-permute-start(bf16[2304,32]{0,1:T(8,128)(2,1)} %convert.74), channel_id=1, source_target_pairs={{0,3},{1,4},{2,5},{3,6},{4,7},{5,8},{6,9},{7,10},{8,11},{9,12},{10... | collective-permute-start | bytes 442376
  375.1 519.3 %collective-permute-start.8 = (bf16[2304,32]{0,1:T(8,128)(2,1)}, bf16[2304,32]{0,1:T(8,128)(2,1)}, u32[]{:S(2)}, u32[]{:S(2)}) collective-permute-start(bf16[2304,32]{0,1:T(8,128)(2,1)} %convert.74), channel_id=1, source_target_pairs={{0,1},{1,2},{2,3},{3,4},{4,5},{5,6},{6,7},{7,8},{8,9},{9,10},{10,1... | collective-permute-start | bytes 442376
  377.0 536.6 %collective-permute-start.9 = (bf16[2304,32]{0,1:T(8,128)(2,1)}, bf16[2304,32]{0,1:T(8,128)(2,1)}, u32[]{:S(2)}, u32[]{:S(2)}) collective-permute-start(bf16[2304,32]{0,1:T(8,128)(2,1)} %convert.74), channel_id=1, source_target_pairs={{0,2},{1,3},{2,4},{3,5},{4,6},{5,7},{6,8},{7,9},{8,10},{9,11},{10,... | collective-permute-start | bytes 442376
  614.0 346.9 %reduce-scatter.21.cloned.1.call-start = ((), (), s32[]{:S(2)}) async-start(), calls=%async_computation.8 | async-start | bytes 8515584
  614.1 277.6 %collective-permute-start.11 = (bf16[2304,28]{0,1:T(8,128)(2,1)S(1)}, bf16[2304,28]{0,1:T(8,128)(2,1)S(1)}, u32[]{:S(2)}, u32[]{:S(2)}) collective-permute-start(bf16[2304,28]{0,1:T(8,128)(2,1)S(1)} %copy-done.17), channel_id=1, source_target_pairs={{0,4},{1,5},{2,6},{3,7},{4,8},{5,9},{6,10},{7,11},{8,12},{9,13},{1... | collective-permute-start | bytes 387080
  615.7 308.0 %collective-permute-start.12 = (bf16[2304,32]{0,1:T(8,128)(2,1)S(1)}, bf16[2304,32]{0,1:T(8,128)(2,1)S(1)}, u32[]{:S(2)}, u32[]{:S(2)}) collective-permute-start(bf16[2304,32]{0,1:T(8,128)(2,1)S(1)} %convert.75), channel_id=1, source_target_pairs={{0,1},{1,2},{2,3},{3,4},{4,5},{5,6},{6,7},{7,8},{8,9},{9,10},{10,1... | collective-permute-start | bytes 442376
  891.7 34.0 %collective-permute-start.13 = (bf16[2304,32]{0,1:T(8,128)(2,1)S(1)}, bf16[2304,32]{0,1:T(8,128)(2,1)S(1)}, u32[]{:S(2)}, u32[]{:S(2)}) collective-permute-start(bf16[2304,32]{0,1:T(8,128)(2,1)S(1)} %convert.75), channel_id=1, source_target_pairs={{0,2},{1,3},{2,4},{3,5},{4,6},{5,7},{6,8},{7,9},{8,10},{9,11},{10,... | collective-permute-start | bytes 442376
  893.0 34.0 %collective-permute-start.14 = (bf16[2304,32]{0,1:T(8,128)(2,1)S(1)}, bf16[2304,32]{0,1:T(8,128)(2,1)S(1)}, u32[]{:S(2)}, u32[]{:S(2)}) collective-permute-start(bf16[2304,32]{0,1:T(8,128)(2,1)S(1)} %convert.75), channel_id=1, source_target_pairs={{0,3},{1,4},{2,5},{3,6},{4,7},{5,8},{6,9},{7,10},{8,11},{9,12},{10... | collective-permute-start | bytes 442376
  894.4 27.7 %collective-permute-start.15 = (bf16[2304,28]{0,1:T(8,128)(2,1)S(1)}, bf16[2304,28]{0,1:T(8,128)(2,1)S(1)}, u32[]{:S(2)}, u32[]{:S(2)}) collective-permute-start(bf16[2304,28]{0,1:T(8,128)(2,1)S(1)} %copy-done.16), channel_id=1, source_target_pairs={{0,4},{1,5},{2,6},{3,7},{4,8},{5,9},{6,10},{7,11},{8,12},{9,13},{1... | collective-permute-start | bytes 387080
  913.7 19.6 %collective-permute-start = (bf16[2304,32]{0,1:T(8,128)(2,1)}, bf16[2304,32]{0,1:T(8,128)(2,1)S(1)}, u32[]{:S(2)}, u32[]{:S(2)}) collective-permute-start(bf16[2304,32]{0,1:T(8,128)(2,1)} %convert.76), channel_id=1, source_target_pairs={{0,1},{1,2},{2,3},{3,4},{4,5},{5,6},{6,7},{7,8},{8,9},{9,10},{10,1... | collective-permute-start | bytes 442376
  922.1 22.7 %collective-permute-start.1 = (bf16[2304,32]{0,1:T(8,128)(2,1)}, bf16[2304,32]{0,1:T(8,128)(2,1)S(1)}, u32[]{:S(2)}, u32[]{:S(2)}) collective-permute-start(bf16[2304,32]{0,1:T(8,128)(2,1)} %convert.76), channel_id=1, source_target_pairs={{0,2},{1,3},{2,4},{3,5},{4,6},{5,7},{6,8},{7,9},{8,10},{9,11},{10,... | collective-permute-start | bytes 442376
  923.7 30.2 %collective-permute-start.2 = (bf16[2304,32]{0,1:T(8,128)(2,1)}, bf16[2304,32]{0,1:T(8,128)(2,1)}, u32[]{:S(2)}, u32[]{:S(2)}) collective-permute-start(bf16[2304,32]{0,1:T(8,128)(2,1)} %convert.76), channel_id=1, source_target_pairs={{0,3},{1,4},{2,5},{3,6},{4,7},{5,8},{6,9},{7,10},{8,11},{9,12},{10... | collective-permute-start | bytes 442376
  925.7 6.2 collective-permute-start.3
  927.0 30.5 %collective-permute-start.4 = (bf16[2304,32]{0,1:T(8,128)(2,1)}, bf16[2304,32]{0,1:T(8,128)(2,1)S(1)}, u32[]{:S(2)}, u32[]{:S(2)}) collective-permute-start(bf16[2304,32]{0,1:T(8,128)(2,1)} %convert.77), channel_id=1, source_target_pairs={{0,1},{1,2},{2,3},{3,4},{4,5},{5,6},{6,7},{7,8},{8,9},{9,10},{10,1... | collective-permute-start | bytes 442376
  931.9 25.7 %collective-permute-start.5 = (bf16[2304,32]{0,1:T(8,128)(2,1)}, bf16[2304,32]{0,1:T(8,128)(2,1)S(1)}, u32[]{:S(2)}, u32[]{:S(2)}) collective-permute-start(bf16[2304,32]{0,1:T(8,128)(2,1)} %convert.77), channel_id=1, source_target_pairs={{0,2},{1,3},{2,4},{3,5},{4,6},{5,7},{6,8},{7,9},{8,10},{9,11},{10,... | collective-permute-start | bytes 442376
  933.2 24.3 %collective-permute-start.6 = (bf16[2304,32]{0,1:T(8,128)(2,1)}, bf16[2304,32]{0,1:T(8,128)(2,1)S(1)}, u32[]{:S(2)}, u32[]{:S(2)}) collective-permute-start(bf16[2304,32]{0,1:T(8,128)(2,1)} %convert.77), channel_id=1, source_target_pairs={{0,3},{1,4},{2,5},{3,6},{4,7},{5,8},{6,9},{7,10},{8,11},{9,12},{10... | collective-permute-start | bytes 442376
  944.9 12.7 %collective-permute-start.7 = (bf16[2304,28]{0,1:T(8,128)(2,1)}, bf16[2304,28]{0,1:T(8,128)(2,1)S(1)}, u32[]{:S(2)}, u32[]{:S(2)}) collective-permute-start(bf16[2304,28]{0,1:T(8,128)(2,1)} %slice.25), channel_id=1, source_target_pairs={{0,4},{1,5},{2,6},{3,7},{4,8},{5,9},{6,10},{7,11},{8,12},{9,13},{1... | collective-permute-start | bytes 387080
  (27 other events, 661.0 us)
Sparse Core Ops, SparseCore 0:
  10.2 51.3 all-gather.29
  64.3 46.5 all-gather.31
  113.0 40.1 all-gather.33
  155.1 40.0 all-gather.37
  197.8 46.4 all-gather.35
  246.8 47.5 all-gather.39
  614.1 84.4 reduce-scatter.22
  755.1 93.8 reduce-scatter.20
where the time goes:
time: 984 us; the launch traced here: 970 us
  blocking collectives  372 us (38%)
  matrix products  281 us (29%)
  waiting for transfers between devices  134 us (14%)
  other arithmetic  76.5 us (8%)
  local copies, waits for them, and re-layouts  45.4 us (5%)
  starting transfers between devices  45.3 us (5%)
  between operations  15.2 us (2%)
    unnamed x4, blocking collectives  372 us
    squeeze x6, waiting for transfers between devices, stack(): h = layer(h, {name: w[number] for name, w in weights.items()})  132 us
    dot_general x6, matrix products, layer(): up = jnp.dot(a, w['w_up'], preferred_element_type=jnp.float32)  105 us
    dot_general x6, matrix products, layer(): gate = jnp.dot(a, w['w_gate'], preferred_element_type=jnp.float32)  95.4 us
    dot_general x5, matrix products, matmul(): jnp.dot(a, w, preferred_element_type=jnp.float32).astype(jnp.bfloat16)  80.4 us
    unnamed x8, other arithmetic  58.7 us
    unnamed x18, starting transfers between devices  44.9 us
    unnamed x67, local copies, waits for them, and re-layouts  38.9 us
  transfers between devices with their start and end apart: 24, of which 5 were waited for; matrix products, arithmetic and copies ran while one was open for 79% of the time, Pallas kernels for 0%

commit v1 on v0

v1 whole, which is shorter than its diff:
```python
import functools
import math
import jax
import jax.numpy as jnp
from jax import lax
from jax.experimental import pallas as pl
from jax.experimental.pallas import tpu as pltpu
from jax.sharding import PartitionSpec as P

MESH = pl.DeviceIdType.MESH
F32, BF16 = jnp.float32, jnp.bfloat16
ALL = slice(None)


def halves(n):
    first = (n // 128 + 1) // 2 * 128
    return (0, first), (first, n - first)


class Place:
    def __init__(self, n):
        self.side = math.isqrt(n // 2)
        me = lax.axis_index("dp")
        chip = me // 2
        self.c = me % 2
        self.xy = (chip // self.side, chip % self.side)
        self.partner = {"dp": chip * 2 + 1 - self.c}

    def hop(self, axis, by):
        xy = list(self.xy)
        xy[axis] = lax.rem(xy[axis] + by + self.side, self.side)
        return {"dp": (xy[0] * self.side + xy[1]) * 2 + self.c}

    def at(self, axis, by):
        return lax.rem(self.xy[axis] + by + self.side, self.side)

    def greet(self):
        barrier = pltpu.get_barrier_semaphore()
        others = [self.partner] + [self.hop(a, d) for a in (0, 1) for d in (1, -1)]
        for other in others:
            pl.semaphore_signal(barrier, inc=1, device_id=other, device_id_type=MESH)
        pl.semaphore_wait(barrier, len(others))


class Sems:
    def __init__(self, send, recv):
        self.send, self.recv, self.used, self.started = send, recv, 0, []

    def copy(self, src, dst, to):
        k = self.used
        self.used += 1
        made = pltpu.make_async_remote_copy(
            src_ref=src, dst_ref=dst, send_sem=self.send.at[k], recv_sem=self.recv.at[k], device_id=to, device_id_type=MESH
        )
        made.start()
        self.started.append(made)
        return made

    def finish(self):
        for made in self.started:
            made.wait_send()


def order(axis, a, b):
    return (a, b) if axis == 0 else (b, a)


class Gather:
    def __init__(self, place, sems, view, other_view, own, axis, lanes):
        self.place, self.sems, self.view, self.other, self.own, self.axis, self.lanes = place, sems, view, other_view, own, axis, lanes

    def a1(self):
        p, q = self.place.at(self.axis, 0), self.place.at(1 - self.axis, 0)
        mine = self.view(*order(self.axis, p, q), None)
        self.sent_a = [self.sems.copy(self.own, mine, self.place.hop(self.axis, d)) for d in (1, -1)]

    def a2(self):
        q = self.place.at(1 - self.axis, 0)
        self.fwd_a = []
        for copy, d, part in zip(self.sent_a, (1, -1), halves(self.lanes), strict=True):
            copy.wait_recv()
            got = self.view(*order(self.axis, self.place.at(self.axis, -d), q), part)
            self.fwd_a.append(self.sems.copy(got, got, self.place.hop(self.axis, d)))

    def slab(self, q, half=None):
        n = self.place.side
        run = pl.ds(0, n) if half is None else pl.ds(half * (n // 2), n // 2)
        return self.view(*order(self.axis, run, q), None)

    def b1(self):
        for copy in self.fwd_a:
            copy.wait_recv()
        mine = self.slab(self.place.at(1 - self.axis, 0))
        self.sent_b = [self.sems.copy(mine, mine, self.place.hop(1 - self.axis, d)) for d in (1, -1)]
        self.to_partner = [self.sems.copy(mine, mine, self.place.partner)]

    def b2(self):
        self.fwd_b = []
        for copy, d, half in zip(self.sent_b, (1, -1), (0, 1), strict=True):
            copy.wait_recv()
            q = self.place.at(1 - self.axis, -d)
            got = self.slab(q, half)
            self.fwd_b.append(self.sems.copy(got, got, self.place.hop(1 - self.axis, d)))
            whole = self.slab(q)
            self.to_partner.append(self.sems.copy(whole, whole, self.place.partner))

    def c1(self):
        for copy, d, half in zip(self.fwd_b, (1, -1), (0, 1), strict=True):
            copy.wait_recv()
            got = self.slab(self.place.at(1 - self.axis, -2 * d), half)
            self.to_partner.append(self.sems.copy(got, got, self.place.partner))

    def end(self):
        for copy in self.to_partner:
            copy.wait_recv()


COPIES = 13


def gather_phases(place, send, recv, local, shards, outs, praw, blk, layers):
    wg, wu, wd = shards
    c = place.c
    sems = Sems(send, recv)
    half = wg.shape[-1] // 2
    rows = wg.shape[1]
    flows, raws, copies = [], [], []

    def p0():
        for j, w in enumerate((wg, wu)):
            raws.append(sems.copy(w, praw.at[j], place.partner))

    def down_rows():
        n = wd.shape[1]
        first = (n // 8 + 1) // 2 * 8
        return ((0, first), (first, n - first))

    def p1():
        x, y = place.xy
        for k, l in enumerate(layers):
            for j, (lo, n) in enumerate(down_rows()):
                def view(xs, ys, part, k=k, lo=lo, n=n):
                    lanes = ALL if part is None else pl.ds(*part)
                    return outs[2].at[k, xs, ys, c, pl.ds(lo, n), lanes]
                own = wd.at[l, pl.ds(lo, n)]
                copies.append(pltpu.make_async_copy(own, view(x, y, None), local.at[len(copies)]))
                copies[-1].start()
                flows.append(Gather(place, sems, view, None, own, j, wd.shape[-1]))
                flows[-1].a1()
        for j, w in enumerate((wg, wu)):
            raws[j].wait_recv()
            for k, l in enumerate(layers):
                for cc in (0, 1):
                    @pl.when(c == cc)
                    def _(cc=cc, j=j, w=w, k=k, l=l):
                        cols = slice(cc * half, (cc + 1) * half)
                        both = (w[l, :, cols].astype(F32), praw[j, l, :, cols].astype(F32))
                        blk[j, k] = jnp.concatenate(both if cc == 0 else both[::-1], axis=0).astype(BF16)
        for k, l in enumerate(layers):
            for j in (0, 1):
                def view(xs, ys, part, k=k, j=j):
                    lo, n = (0, half) if part is None else part
                    lanes = pl.ds(pl.multiple_of(c * half + lo, 128), n)
                    return outs[j].at[k, xs, ys, :, lanes]
                own = blk.at[j, k]
                copies.append(pltpu.make_async_copy(own, view(x, y, None), local.at[len(copies)]))
                copies[-1].start()
                flows.append(Gather(place, sems, view, None, own, j, half))
                flows[-1].a1()

    def every(step):
        def run():
            for flow in flows:
                getattr(flow, step)()
        return run

    def b1():
        for copy in copies:
            copy.wait()
        every("b1")()

    def end():
        every("end")()
        sems.finish()

    return [p0, p1, every("a2"), b1, every("b2"), every("c1"), end]


def gather(n, layers, wg, wu, wd, cid):
    side = math.isqrt(n // 2)
    L, rows, F = wg.shape
    drows, D = wd.shape[1:]
    k = len(layers)
    count = 2 + 4 * k * COPIES

    def kernel(wg, wu, wd, og, ou, od, praw, blk, send, recv, local):
        place = Place(n)
        place.greet()
        for phase in gather_phases(place, send, recv, local, (wg, wu, wd), (og, ou, od), praw, blk, layers):
            phase()

    out = pl.pallas_call(
        kernel,
        out_shape=[jax.ShapeDtypeStruct((k, side, side, 2 * rows, F), BF16)] * 2
        + [jax.ShapeDtypeStruct((k, side, side, 2, drows, D), BF16)],
        in_specs=[pl.BlockSpec(memory_space=pltpu.VMEM)] * 2 + [pl.BlockSpec(memory_space=pltpu.HBM)],
        out_specs=[pl.BlockSpec(memory_space=pltpu.HBM)] * 3,
        scratch_shapes=[
            pltpu.VMEM((2, L, rows, F), BF16),
            pltpu.VMEM((2, k, 2 * rows, F // 2), BF16),
            pltpu.SemaphoreType.DMA((count,)),
            pltpu.SemaphoreType.DMA((count,)),
            pltpu.SemaphoreType.DMA((4 * k,)),
        ],
        compiler_params=pltpu.CompilerParams(collective_id=cid, has_side_effects=True, vmem_limit_bytes=60 << 20),
        name=f"gather{cid}",
    )(wg, wu, wd)
    return [t.reshape(k, n * rows, F) for t in out[:2]] + [out[2].reshape(k, n * drows, D)]


class Scatter:
    def __init__(self, place, sems, axis, own, l1, part_a, full_a, total, snd_b, part_b, full_b):
        self.place, self.sems, self.axis = place, sems, axis
        self.own, self.l1, self.part_a, self.full_a, self.total, self.snd_b, self.part_b, self.full_b = (
            own, l1, part_a, full_a, total, snd_b, part_b, full_b)
        self.w = own.shape[-1]

    def idx(self, a, b):
        return order(self.axis, a, b)

    def pair(self, a, b):
        i = self.idx(a, b)
        return self.own[i].astype(F32) + self.l1[i].astype(F32)

    def loop(self, lo, n, body):
        lax.fori_loop(lo, lo + n, lambda j, _: (body(j), 0)[1], 0)

    def a1(self):
        n = self.place.side
        far = self.place.at(self.axis, 2)

        def body(j):
            self.own[self.idx(far, j)] = self.pair(far, j).astype(BF16)

        self.loop(0, n, body)
        self.sent_a = [
            self.sems.copy(self.own.at[self.idx(far, pl.ds(h * (n // 2), n // 2))], self.part_a.at[h], self.place.hop(self.axis, d))
            for h, d in enumerate((1, -1))
        ]

    def a2(self):
        n = self.place.side
        self.fwd_a = []
        for h, d in enumerate((1, -1)):
            to = self.place.at(self.axis, d)
            lo, rest = h * (n // 2), (1 - h) * (n // 2)

            def plain(j, to=to):
                self.own[self.idx(to, j)] = self.pair(to, j).astype(BF16)

            self.loop(rest, n // 2, plain)
            self.sent_a[h].wait_recv()

            def added(j, to=to, h=h, lo=lo):
                self.own[self.idx(to, j)] = (self.pair(to, j) + self.part_a[h, j - lo].astype(F32)).astype(BF16)

            self.loop(lo, n // 2, added)
            self.fwd_a.append(self.sems.copy(self.own.at[self.idx(to, pl.ds(0, n))], self.full_a.at[h], self.place.hop(self.axis, d)))

    def b1(self):
        n = self.place.side
        p = self.place.at(self.axis, 0)
        for copy in self.fwd_a:
            copy.wait_recv()

        def body(j):
            self.total[j] = self.pair(p, j) + self.full_a[0, j].astype(F32) + self.full_a[1, j].astype(F32)

        self.loop(0, n, body)
        far = self.place.at(1 - self.axis, 2)
        self.snd_b[far] = self.total[far].astype(BF16)
        self.sent_b = [
            self.sems.copy(self.snd_b.at[far, :, pl.ds(*part)], self.part_b.at[h, :, pl.ds(*part)], self.place.hop(1 - self.axis, d))
            for h, (d, part) in enumerate(zip((1, -1), halves(self.w), strict=True))
        ]

    def b2(self):
        self.fwd_b = []
        for h, (d, part) in enumerate(zip((1, -1), halves(self.w), strict=True)):
            to = self.place.at(1 - self.axis, d)
            lo, w = part
            rest = slice(w, self.w) if lo == 0 else slice(0, lo)
            got = slice(lo, lo + w)
            self.snd_b[to, :, rest] = self.total[to, :, rest].astype(BF16)
            self.sent_b[h].wait_recv()
            self.snd_b[to, :, got] = (self.total[to, :, got] + self.part_b[h, :, got].astype(F32)).astype(BF16)
            self.fwd_b.append(self.sems.copy(self.snd_b.at[to], self.full_b.at[h], self.place.hop(1 - self.axis, d)))

    def last(self):
        for copy in self.fwd_b:
            copy.wait_recv()
        return self.total[self.place.at(1 - self.axis, 0)] + self.full_b[0].astype(F32) + self.full_b[1].astype(F32)


def scatter_scratch(side, r, w):
    return [
        pltpu.VMEM((side, side, r, w), BF16),
        pltpu.VMEM((side, side, r, w), BF16),
        pltpu.VMEM((2, side // 2, r, w), BF16),
        pltpu.VMEM((2, side, r, w), BF16),
        pltpu.VMEM((side, r, w), F32),
        pltpu.VMEM((side, r, w), BF16),
        pltpu.VMEM((2, r, w), BF16),
        pltpu.VMEM((2, r, w), BF16),
    ]


def down_split(drows):
    first = (drows // 8 + 1) // 2 * 8
    return ((0, first), (first, drows - first))


def scatter_phases(place, send, recv, local, terms, outs, swap, bufs):
    c = place.c
    sems = Sems(send, recv)
    half = terms[0].shape[-1] // 2
    drows = terms[2].shape[3]
    (lo0, n0), (lo1, n1) = down_split(drows)

    def cols(j, who):
        return terms[j].at[:, :, :, pl.ds(pl.multiple_of(who * half, 128), half)]

    def share(who):
        return [
            terms[2].at[:, :, who, pl.ds(lo0, n0), :],
            terms[2].at[:, :, who, pl.ds(lo1, n1), :],
            cols(0, who),
            cols(1, who),
        ]

    axes = (0, 1, 0, 1)
    flows = [Scatter(place, sems, axis, *buf) for axis, buf in zip(axes, bufs, strict=True)]
    first, loads = [], []

    def p0():
        for k, (mine, theirs, flow) in enumerate(zip(share(c), share(1 - c), flows, strict=True)):
            first.append(sems.copy(theirs, flow.l1, place.partner))
            loads.append(pltpu.make_async_copy(mine, flow.own, local.at[k]))
            loads[-1].start()

    def a1():
        for flow, got, load in zip(flows, first, loads, strict=True):
            load.wait()
            got.wait_recv()
            flow.a1()

    def every(step):
        def run():
            for flow in flows:
                getattr(flow, step)()
        return run

    def end():
        rows = outs[0].shape[0]
        outs[2][pl.ds(lo0, n0), :] = flows[0].last().astype(BF16)
        outs[2][pl.ds(lo1, n1), :] = flows[1].last().astype(BF16)
        swaps = []
        for j in (0, 1):
            block = flows[2 + j].last()
            parts = (block[:rows].astype(BF16), block[rows:].astype(BF16))
            for cc in (0, 1):
                @pl.when(c == cc)
                def _(cc=cc, parts=parts, j=j):
                    outs[j][:, cc * half : (cc + 1) * half] = parts[cc]
                    swap[j] = parts[1 - cc]
            lanes = pl.ds(pl.multiple_of(c * half, 128), half)
            swaps.append(sems.copy(swap.at[j], outs[j].at[:, lanes], place.partner))
        for copy in swaps:
            copy.wait_recv()
        sems.finish()

    return [p0, a1, every("a2"), every("b1"), every("b2"), end]


def scatter(n, dwg, dwu, dwd, cid):
    side = math.isqrt(n // 2)
    D, F = dwg.shape
    rows, drows = D // n, F // n
    (_, n0), (_, n1) = down_split(drows)
    shapes = [(n0, D), (n1, D), (2 * rows, F // 2), (2 * rows, F // 2)]
    scratch = [scatter_scratch(side, r, w) for r, w in shapes]
    each = len(scratch[0])
    count = 4 * 9 + 2

    def kernel(dwg, dwu, dwd, og, ou, od, swap, send, recv, local, *flat):
        place = Place(n)
        place.greet()
        bufs = [flat[i * each : (i + 1) * each] for i in range(4)]
        for phase in scatter_phases(place, send, recv, local, (dwg, dwu, dwd), (og, ou, od), swap, bufs):
            phase()

    return pl.pallas_call(
        kernel,
        out_shape=[jax.ShapeDtypeStruct((rows, F), BF16)] * 2 + [jax.ShapeDtypeStruct((drows, D), BF16)],
        in_specs=[pl.BlockSpec(memory_space=pltpu.HBM)] * 3,
        out_specs=[pl.BlockSpec(memory_space=pltpu.VMEM)] * 3,
        scratch_shapes=[
            pltpu.VMEM((2, rows, F // 2), BF16),
            pltpu.SemaphoreType.DMA((count,)),
            pltpu.SemaphoreType.DMA((count,)),
            pltpu.SemaphoreType.DMA((4,)),
        ]
        + [s for group in scratch for s in group],
        compiler_params=pltpu.CompilerParams(collective_id=cid, has_side_effects=True, vmem_limit_bytes=60 << 20),
        name=f"scatter{cid}",
    )(dwg.reshape(side, side, 2 * rows, F), dwu.reshape(side, side, 2 * rows, F), dwd.reshape(side, side, 2, drows, D))


def dot(a, b, dims=((1,), (0,))):
    return lax.dot_general(a, b, (dims, ((), ())), preferred_element_type=F32)


def normed(h):
    wide = h.astype(F32)
    scale = lax.rsqrt(jnp.mean(wide**2, -1, keepdims=True) + 1e-6)
    return (wide * scale).astype(BF16)


def layer(h, wg, wu, wd):
    a = normed(h)
    gate, up = dot(a, wg), dot(a, wu)
    return h + dot((jax.nn.silu(gate) * up).astype(BF16), wd).astype(BF16)


def solution(mesh):
    n = mesh.shape["dp"]

    def device(x, dy, wg, wu, wd):
        layers = range(wg.shape[0])
        gg, gu, gd = gather(n, tuple(layers), wg, wu, wd, 0)

        def stack(weights, h):
            for w in weights:
                h = layer(h, *w)
            return h

        weights = [(gg[l], gu[l], gd[l]) for l in layers]
        _, back = jax.vjp(stack, weights, x[0])
        by_weights, by_x = back(dy[0])
        parts = [scatter(n, *by_weights[l], 1) for l in reversed(layers)][::-1]
        return (by_x[None], *(jnp.stack([p[j] for p in parts]) for j in range(3)))

    tokens, rows = P(("rep", "dp")), P(None, "dp")
    return jax.shard_map(
        device, mesh=mesh, in_specs=(tokens, tokens, rows, rows, rows), out_specs=(tokens, *[P("rep", "dp")] * 3), check_vma=False
    )
```

time: 984 us -> 522 us (0.53)
  blocking collectives: 372 us -> 0 us
  Pallas kernels: 0 us -> 173 us
  waiting for transfers between devices: 134 us -> 0 us
  other arithmetic: 76.5 us -> 14 us
  starting transfers between devices: 45.3 us -> 0 us
  between operations: 15.2 us -> 1.12 us
    unnamed x4 -> x0, blocking collectives: 372 us -> none
    pallas_call x0 -> x3, Pallas kernels: none -> 173 us  [the longest x2 94.1 us: scatter(): pl.pallas_call(kernel, out_shape=[jax.ShapeDtypeStruct((rows, F), BF16)]...]
    squeeze x6 -> x0, waiting for transfers between devices: 132 us -> none  [stack(): h = layer(h, {name: w[number] for name, w in weights.items()})]
    unnamed x8 -> x0, other arithmetic: 58.7 us -> none
    unnamed x18 -> x0, starting transfers between devices: 44.9 us -> none
    unnamed x67 -> x53, local copies, waits for them, and re-layouts: 38.9 us -> 29.2 us
  transfers between devices with their start and end apart: 24 -> 0, of which waited for: 5 -> 0; matrix products, arithmetic and copies ran while one was open for 79% -> 0% of each run, Pallas kernels for 0% -> 0%
where the time goes in v1:
time: 522 us; the launch traced here: 517 us
  matrix products  286 us (55%)
  Pallas kernels  173 us (33%)
  local copies, waits for them, and re-layouts  43.2 us (8%)
  other arithmetic  14 us (3%)
    dot_general x17, matrix products, dot(): return lax.dot_general(a, b, (dims, ((), ())), preferred_element_type=F32)  286 us
    pallas_call x2, Pallas kernels, scatter(): pl.pallas_call(kernel, out_shape=[jax.ShapeDtypeStruct((rows, F), BF16)]...  94.1 us
    pallas_call x1, Pallas kernels, gather(): pl.pallas_call(kernel, out_shape=[jax.ShapeDtypeStruct((k, side, side, 2...  79.1 us
    unnamed x53, local copies, waits for them, and re-layouts  29.2 us
    slice x2, local copies, waits for them, and re-layouts, device(): weights = [(gg[l], gu[l], gd[l]) for l in layers]  14 us

profile of v1, /device:TPU:97, one launch (start us, length us, event | category | flops | bytes accessed | tf_op | source)
XLA Modules:
  0.0 517.2 jit_solution(14741829352012080992)
XLA Ops:
  4.1 6.0 %copy.10 = bf16[1,2048,896]{1,2,0:T(8,128)(2,1)} copy(bf16[1,2048,896]{2,1,0:T(8,128)(2,1)} %param.5) | data formatting | bytes 7340032 | tf_op args[0]
  13.5 6.2 %copy.9 = bf16[1,2048,896]{1,2,0:T(8,128)(2,1)} copy(bf16[1,2048,896]{2,1,0:T(8,128)(2,1)} %param.6) | data formatting | bytes 7340032 | tf_op args[1]
  19.7 79.1 %gather0.1 = (bf16[2,4,4,56,2304]{4,3,2,1,0:T(8,128)(2,1)}, bf16[2,4,4,56,2304]{4,3,2,1,0:T(8,128)(2,1)}, bf16[2,4,4,2,72,896]{5,4,3,2,1,0:T(8,128)(2,1)}) custom-call(bf16[2,28,2304]{2,1,0:T(8,128)(2,1)} %copy.11.wg, bf16[2,28,2304]{2,1,0:T(8,128)(2,1)} %copy.12.wu, bf16[2,72,896]{2,1,0:T(8,128)(2,1)} %wd.1), custom_call_target="tpu_custom_call" | custom-call | tf_op jit(solution)/shard_map/gather0/pallas_call | solution.py:202
  98.8 11.6 %fusion.49 = (bf16[1,4,4,56,2304]{4,3,2,1,0:T(8,128)(2,1)}, bf16[1,4,4,56,2304]{4,3,2,1,0:T(8,128)(2,1)S(1)}, bf16[1,4,4,56,2304]{4,3,2,1,0:T(8,128)(2,1)}, bf16[1,4,4,56,2304]{4,3,2,1,0:T(8,128)(2,1)}) fusion(bf16[2,4,4,56,2304]{4,3,2,1,0:T(8,128)(2,1)} %get-tuple-element.13, bf16[2,4,4,56,2304]{4,3,2,1,0:T(8,128)(2,1)} %get-tuple-element.14), kind=kLoop, calls=%fused_computation.72 | loop fusion | bytes 33030144 | tf_op jit(solution)/shard_map/slice | solution.py:447
  115.3 12.3 %convolution_convert_fusion.1 = bf16[2304,2048]{0,1:T(8,128)(2,1)} fusion(bf16[2304,896]{1,0:T(8,128)(2,1)S(1)} %bitcast.78, bf16[1,2048,896]{2,1,0:T(8,128)(2,1)S(1)} %copy-done.11), kind=kOutput, calls=%fused_computation.29 | convolution fusion | flops 8460435456 | bytes 17235968 | tf_op jit(solution)/shard_map/transpose(jvp())/dot_general | solution.py:420
  127.6 13.2 %fusion.40 = f32[2048,2304]{1,0:T(8,128)} fusion(bf16[896,2304]{1,0:T(8,128)(2,1)S(1)} %bitcast.79, bf16[1,2048,896]{2,1,0:T(8,128)(2,1)S(1)} %copy-done.10, f32[2048]{0:T(1024)S(1)} %fusion.42), kind=kOutput, calls=%fused_computation.62 | convolution fusion | flops 8461221888 | bytes 26681344 | tf_op jit(solution)/shard_map/jvp()/dot_general | solution.py:420
  140.8 21.3 %multiply_convert_fusion.1 = (bf16[2048,2304]{1,0:T(8,128)(2,1)}, f32[2048,2304]{1,0:T(8,128)}) fusion(f32[2048,2304]{1,0:T(8,128)} %fusion.40, bf16[896,2304]{1,0:T(8,128)(2,1)} %bitcast.81, bf16[1,2048,896]{2,1,0:T(8,128)(2,1)} %param.5, f32[2048]{0:T(1024)S(1)} %fusion.42), kind=kOutput, calls=%fused_computation.13 | convolution fusion | flops 8489533440 | bytes 54992896 | tf_op jit(solution)/shard_map/jvp()/dot_general | solution.py:420
  162.1 14.0 %fusion.18 = (f32[2048]{0:T(1024)S(1)}, bf16[2048,896]{0,1:T(8,128)(2,1)S(1)}) fusion(bf16[2048,2304]{1,0:T(8,128)(2,1)} %get-tuple-element.32, bf16[2304,896]{1,0:T(8,128)(2,1)} %bitcast.76, bf16[1,2048,896]{1,2,0:T(8,128)(2,1)} %copy.10), kind=kOutput, calls=%fused_computation.40 | convolution fusion | flops 8464889856 | bytes 20914176 | tf_op jit(solution)/shard_map/jvp()/dot_general | solution.py:420
  176.7 13.6 %fusion.34 = f32[2048,2304]{1,0:T(8,128)} fusion(bf16[896,2304]{1,0:T(8,128)(2,1)S(1)} %bitcast.86, bf16[2048,896]{0,1:T(8,128)(2,1)S(1)} %get-tuple-element.35, f32[2048]{0:T(1024)S(1)} %fusion.43), kind=kOutput, calls=%fused_computation.59 | convolution fusion | flops 8461221888 | bytes 26681344 | tf_op jit(solution)/shard_map/jvp()/dot_general | solution.py:420
  190.3 25.5 %fusion.1 = (bf16[2048,2304]{1,0:T(8,128)(2,1)}, f32[2048,2304]{1,0:T(8,128)}) fusion(f32[2048,2304]{1,0:T(8,128)} %fusion.34, bf16[2304,2048]{0,1:T(8,128)(2,1)} %convolution_convert_fusion.1, bf16[896,2304]{1,0:T(8,128)(2,1)S(1)} %bitcast.83, bf16[2048,896]{0,1:T(8,128)(2,1)S(1)} %get-tuple-element.35, f32[2048]{0:T(1024)S(1)} %fusion.43), kind=kOutput, calls=%fused_computation.5 | convolution fusion | flops 8517844992 | bytes 64430080 | tf_op jit(solution)/shard_map/jvp()/dot_general | solution.py:420
  215.9 19.5 %fusion.21 = bf16[2304,896]{1,0:T(8,128)(2,1)} fusion(f32[2048,2304]{1,0:T(8,128)} %fusion.34, bf16[1,2048,896]{2,1,0:T(8,128)(2,1)} %param.6, f32[2048,2304]{1,0:T(8,128)} %get-tuple-element.37), kind=kOutput, calls=%fused_computation.44 | convolution fusion | flops 8486092800 | bytes 45547520 | tf_op jit(solution)/shard_map/transpose(jvp())/dot_general | solution.py:420
  235.4 17.0 %fusion.7 = bf16[2048,896]{0,1:T(8,128)(2,1)} fusion(bf16[896,2304]{1,0:T(8,128)(2,1)} %bitcast.85, bf16[2304,2048]{0,1:T(8,128)(2,1)} %convolution_convert_fusion.1, f32[2048,2304]{1,0:T(8,128)} %get-tuple-element.37), kind=kOutput, calls=%fused_computation.17 | convolution fusion | flops 8484028416 | bytes 36110336 | tf_op jit(solution)/shard_map/transpose(jvp())/dot_general | solution.py:420
  252.4 17.1 %fusion.23 = bf16[896,2304]{1,0:T(8,128)(2,1)} fusion(bf16[2304,2048]{0,1:T(8,128)(2,1)} %convolution_convert_fusion.1, bf16[2048,896]{0,1:T(8,128)(2,1)S(1)} %copy-done.13, f32[2048]{0:T(1024)S(1)} %fusion.43, f32[2048,2304]{1,0:T(8,128)} %get-tuple-element.37), kind=kOutput, calls=%fused_computation.46 | convolution fusion | flops 8491597824 | bytes 36118528 | tf_op jit(solution)/shard_map/transpose(jvp())/dot_general | solution.py:420
  269.5 12.5 %fusion.20 = (f32[2048]{0:T(1024)S(1)}, bf16[2048,896]{0,1:T(8,128)(2,1)S(1)}) fusion(bf16[2048,896]{0,1:T(8,128)(2,1)S(1)} %copy-done.13, bf16[2048,896]{0,1:T(8,128)(2,1)} %fusion.7, bf16[2048,2304]{1,0:T(8,128)(2,1)} %get-tuple-element.36, bf16[896,2304]{1,0:T(8,128)(2,1)S(1)} %bitcast.84), kind=kOutput, calls=%fused_computation.42 | convolution fusion | flops 8464889856 | bytes 24584192 | tf_op jit(solution)/shard_map/transpose(jvp())/dot_general | solution.py:420
  282.1 13.7 %convolution_convert_fusion.2 = bf16[896,2304]{1,0:T(8,128)(2,1)} fusion(bf16[2048,2304]{1,0:T(8,128)(2,1)} %get-tuple-element.36, bf16[2048,896]{0,1:T(8,128)(2,1)S(1)} %copy-done.13, f32[2048]{0:T(1024)S(1)} %fusion.43), kind=kOutput, calls=%fused_computation.47 | convolution fusion | flops 8461221888 | bytes 17244160 | tf_op jit(solution)/shard_map/transpose(jvp())/dot_general | solution.py:420
  300.7 14.4 %convolution_convert_fusion.3 = bf16[2304,896]{1,0:T(8,128)(2,1)} fusion(bf16[2048,2304]{1,0:T(8,128)(2,1)} %get-tuple-element.32, bf16[2048,896]{0,1:T(8,128)(2,1)S(1)} %fusion.27), kind=kOutput, calls=%fused_computation.48 | convolution fusion | flops 8457781248 | bytes 17235968 | tf_op jit(solution)/shard_map/transpose(jvp())/dot_general | solution.py:420
  315.1 31.1 %fusion.3 = (bf16[2048,2304]{1,0:T(8,128)(2,1)}, bf16[2048,2304]{1,0:T(8,128)(2,1)}) fusion(f32[2048,2304]{1,0:T(8,128)} %fusion.40, f32[2048,2304]{1,0:T(8,128)} %get-tuple-element.33, bf16[2048,896]{0,1:T(8,128)(2,1)} %copy-done.2, bf16[2304,896]{1,0:T(8,128)(2,1)} %bitcast.77), kind=kOutput, calls=%fused_computation.7 | convolution fusion | flops 8517058560 | bytes 64421888 | tf_op jit(solution)/shard_map/transpose(jvp())/dot_general | solution.py:420
  346.1 17.0 %fusion.9 = bf16[2048,896]{0,1:T(8,128)(2,1)} fusion(bf16[896,2304]{1,0:T(8,128)(2,1)} %bitcast.82, bf16[2048,2304]{1,0:T(8,128)(2,1)} %get-tuple-element.41, f32[2048,2304]{1,0:T(8,128)} %fusion.40), kind=kOutput, calls=%fused_computation.19 | convolution fusion | flops 8484028416 | bytes 36110336 | tf_op jit(solution)/shard_map/transpose(jvp())/dot_general | solution.py:420
  363.2 17.2 %fusion.22 = bf16[896,2304]{1,0:T(8,128)(2,1)} fusion(bf16[2048,2304]{1,0:T(8,128)(2,1)} %get-tuple-element.41, bf16[1,2048,896]{1,2,0:T(8,128)(2,1)S(1)} %copy-done, f32[2048]{0:T(1024)S(1)} %copy-done.20, f32[2048,2304]{1,0:T(8,128)} %fusion.40), kind=kOutput, calls=%fused_computation.45 | convolution fusion | flops 8491597824 | bytes 36118528 | tf_op jit(solution)/shard_map/transpose(jvp())/dot_general | solution.py:420
  380.3 12.5 %fusion.16 = (f32[2048]{0:T(1024)S(1)}, bf16[2048,896]{0,1:T(8,128)(2,1)S(1)}) fusion(bf16[1,2048,896]{1,2,0:T(8,128)(2,1)S(1)} %copy-done, bf16[2048,896]{0,1:T(8,128)(2,1)} %fusion.9, bf16[2048,2304]{1,0:T(8,128)(2,1)} %get-tuple-element.40, bf16[896,2304]{1,0:T(8,128)(2,1)S(1)} %bitcast.80), kind=kOutput, calls=%fused_computation.38 | convolution fusion | flops 8464889856 | bytes 24584192 | tf_op jit(solution)/shard_map/transpose(jvp())/dot_general | solution.py:420
  392.8 13.7 %convolution_convert_fusion.4 = bf16[896,2304]{1,0:T(8,128)(2,1)} fusion(bf16[2048,2304]{1,0:T(8,128)(2,1)} %get-tuple-element.40, bf16[1,2048,896]{1,2,0:T(8,128)(2,1)S(1)} %copy-done, f32[2048]{0:T(1024)S(1)} %copy-done.20), kind=kOutput, calls=%fused_computation.49 | convolution fusion | flops 8461221888 | bytes 17244160 | tf_op jit(solution)/shard_map/transpose(jvp())/dot_general | solution.py:420
  411.3 6.0 %copy.14 = bf16[1,2048,896]{2,1,0:T(8,128)(2,1)} copy(bf16[1,2048,896]{1,2,0:T(8,128)(2,1)} %fusion.26) | data formatting | bytes 7340032
  417.3 46.2 %scatter1.2 = (bf16[28,2304]{1,0:T(8,128)(2,1)}, bf16[28,2304]{1,0:T(8,128)(2,1)}, bf16[72,896]{1,0:T(8,128)(2,1)}) custom-call(bf16[4,4,56,2304]{3,2,1,0:T(8,128)(2,1)} %bitcast.75, bf16[4,4,56,2304]{3,2,1,0:T(8,128)(2,1)} %bitcast.74, bf16[4,4,2,72,896]{4,3,2,1,0:T(8,128)(2,1)} %bitcast.73), custom_call_target="tpu_custom_call" | custom-call | tf_op jit(solution)/shard_map/scatter1/pallas_call | solution.py:402
  463.6 47.9 %scatter1.3 = (bf16[28,2304]{1,0:T(8,128)(2,1)}, bf16[28,2304]{1,0:T(8,128)(2,1)}, bf16[72,896]{1,0:T(8,128)(2,1)}) custom-call(bf16[4,4,56,2304]{3,2,1,0:T(8,128)(2,1)} %bitcast.72, bf16[4,4,56,2304]{3,2,1,0:T(8,128)(2,1)} %bitcast.71, bf16[4,4,2,72,896]{4,3,2,1,0:T(8,128)(2,1)} %bitcast.70), custom_call_target="tpu_custom_call" | custom-call | tf_op jit(solution)/shard_map/scatter1/pallas_call | solution.py:402
  (61 shorter events, 27.4 us)
Async XLA Ops:
  12.9 0.6 copy-start.17
  13.5 127.2 %copy-start.19 = (f32[2048]{0:T(1024)}, f32[2048]{0:T(1024)S(1)}, u32[]{:S(2)}) copy-start(f32[2048]{0:T(1024)S(1)} %fusion.42) | copy-start | bytes 24580
  98.8 12.5 %copy-start.4 = (bf16[2,4,4,2,72,896]{5,4,3,2,1,0:T(8,128)(2,1)S(1)}, bf16[2,4,4,2,72,896]{5,4,3,2,1,0:T(8,128)(2,1)}, u32[]{:S(2)}) copy-start(bf16[2,4,4,2,72,896]{5,4,3,2,1,0:T(8,128)(2,1)} %get-tuple-element.15) | copy-start | bytes 24772612
  110.4 17.2 %copy-start.5 = (bf16[1,4,4,56,2304]{4,3,2,1,0:T(8,128)(2,1)}, bf16[1,4,4,56,2304]{4,3,2,1,0:T(8,128)(2,1)S(1)}, u32[]{:S(2)}) copy-start(bf16[1,4,4,56,2304]{4,3,2,1,0:T(8,128)(2,1)S(1)} %get-tuple-element.27) | copy-start | bytes 12386308
  111.3 4.0 copy-start.11
  115.3 12.3 %copy-start.10 = (bf16[1,2048,896]{2,1,0:T(8,128)(2,1)S(1)}, bf16[1,2048,896]{2,1,0:T(8,128)(2,1)}, u32[]{:S(2)}) copy-start(bf16[1,2048,896]{2,1,0:T(8,128)(2,1)} %param.5) | copy-start | bytes 11010052
  162.1 14.6 %copy-start.9 = (bf16[1,4,4,56,2304]{4,3,2,1,0:T(8,128)(2,1)S(1)}, bf16[1,4,4,56,2304]{4,3,2,1,0:T(8,128)(2,1)}, u32[]{:S(2)}) copy-start(bf16[1,4,4,56,2304]{4,3,2,1,0:T(8,128)(2,1)} %get-tuple-element.45) | copy-start | bytes 12386308
  176.1 0.6 copy-start.21
  176.1 14.2 %copy-start.12 = (bf16[2048,896]{0,1:T(8,128)(2,1)}, bf16[2048,896]{0,1:T(8,128)(2,1)S(1)}, u32[]{:S(2)}) copy-start(bf16[2048,896]{0,1:T(8,128)(2,1)S(1)} %get-tuple-element.35) | copy-start | bytes 11010052
  176.7 13.6 %copy-start.7 = (bf16[1,4,4,56,2304]{4,3,2,1,0:T(8,128)(2,1)S(1)}, bf16[1,4,4,56,2304]{4,3,2,1,0:T(8,128)(2,1)}, u32[]{:S(2)}) copy-start(bf16[1,4,4,56,2304]{4,3,2,1,0:T(8,128)(2,1)} %get-tuple-element.26) | copy-start | bytes 12386308
  235.4 17.0 %copy-start.13 = (bf16[2048,896]{0,1:T(8,128)(2,1)S(1)}, bf16[2048,896]{0,1:T(8,128)(2,1)}, u32[]{:S(2)}) copy-start(bf16[2048,896]{0,1:T(8,128)(2,1)} %copy-done.12) | copy-start | bytes 11010052
  252.4 17.1 %copy-start.8 = (bf16[1,4,4,56,2304]{4,3,2,1,0:T(8,128)(2,1)S(1)}, bf16[1,4,4,56,2304]{4,3,2,1,0:T(8,128)(2,1)}, u32[]{:S(2)}) copy-start(bf16[1,4,4,56,2304]{4,3,2,1,0:T(8,128)(2,1)} %get-tuple-element.26) | copy-start | bytes 12386308
  282.1 13.7 %copy-start.22 = (f32[2048]{0:T(1024)S(1)}, f32[2048]{0:T(1024)}, u32[]{:S(2)}) copy-start(f32[2048]{0:T(1024)} %copy-done.21) | copy-start | bytes 24580
  282.1 13.7 %copy-start.1 = (bf16[1,2048,896]{1,2,0:T(8,128)(2,1)S(1)}, bf16[1,2048,896]{1,2,0:T(8,128)(2,1)}, u32[]{:S(2)}) copy-start(bf16[1,2048,896]{1,2,0:T(8,128)(2,1)} %copy.9) | copy-start | bytes 11010052
  298.8 1.9 copy-start.2
  346.1 17.0 %copy-start = (bf16[1,2048,896]{1,2,0:T(8,128)(2,1)S(1)}, bf16[1,2048,896]{1,2,0:T(8,128)(2,1)}, u32[]{:S(2)}) copy-start(bf16[1,2048,896]{1,2,0:T(8,128)(2,1)} %copy.10) | copy-start | bytes 11010052
  346.1 17.0 %copy-start.20 = (f32[2048]{0:T(1024)S(1)}, f32[2048]{0:T(1024)}, u32[]{:S(2)}) copy-start(f32[2048]{0:T(1024)} %copy-done.19) | copy-start | bytes 24580
  363.1 17.2 %copy-start.6 = (bf16[1,4,4,56,2304]{4,3,2,1,0:T(8,128)(2,1)S(1)}, bf16[1,4,4,56,2304]{4,3,2,1,0:T(8,128)(2,1)}, u32[]{:S(2)}) copy-start(bf16[1,4,4,56,2304]{4,3,2,1,0:T(8,128)(2,1)} %copy-done.5) | copy-start | bytes 12386308
  392.8 13.8 %copy-start.18 = (f32[2048]{0:T(1024)S(1)}, f32[2048]{0:T(1024)}, u32[]{:S(2)}) copy-start(f32[2048]{0:T(1024)} %copy-done.17) | copy-start | bytes 24580
  392.8 13.8 %copy-start.3 = (bf16[2048,896]{0,1:T(8,128)(2,1)S(1)}, bf16[2048,896]{0,1:T(8,128)(2,1)}, u32[]{:S(2)}) copy-start(bf16[2048,896]{0,1:T(8,128)(2,1)} %copy-done.2) | copy-start | bytes 11010052
  463.5 47.9 %copy-start.15 = (bf16[28,2304]{1,0:T(8,128)(2,1)S(1)}, bf16[28,2304]{1,0:T(8,128)(2,1)}, u32[]{:S(2)}) copy-start(bf16[28,2304]{1,0:T(8,128)(2,1)} %get-tuple-element.16) | copy-start | bytes 387076
  463.5 49.8 %copy-start.14 = (bf16[28,2304]{1,0:T(8,128)(2,1)S(1)}, bf16[28,2304]{1,0:T(8,128)(2,1)}, u32[]{:S(2)}) copy-start(bf16[28,2304]{1,0:T(8,128)(2,1)} %get-tuple-element.18) | copy-start | bytes 387076
  463.6 51.7 %copy-start.16 = (bf16[72,896]{1,0:T(8,128)(2,1)S(1)}, bf16[72,896]{1,0:T(8,128)(2,1)}, u32[]{:S(2)}) copy-start(bf16[72,896]{1,0:T(8,128)(2,1)} %get-tuple-element.20) | copy-start | bytes 387076

commit v2 on v1

v2 whole, which is shorter than its diff:
```python
import functools
import math
import jax
import jax.numpy as jnp
from jax import lax
from jax.experimental import pallas as pl
from jax.experimental.pallas import tpu as pltpu
from jax.sharding import PartitionSpec as P

MESH = pl.DeviceIdType.MESH
F32, BF16 = jnp.float32, jnp.bfloat16
ALL = slice(None)


def halves(n):
    first = (n // 128 + 1) // 2 * 128
    return (0, first), (first, n - first)


class Place:
    def __init__(self, n):
        self.side = math.isqrt(n // 2)
        me = lax.axis_index("dp")
        chip = me // 2
        self.c = me % 2
        self.xy = (chip // self.side, chip % self.side)
        self.partner = {"dp": chip * 2 + 1 - self.c}
        self.places = {(a, d): lax.rem(self.xy[a] + d + self.side, self.side) for a in (0, 1) for d in range(-2, 3)}
        self.hops = {}
        for a in (0, 1):
            for d in (1, -1):
                xy = list(self.xy)
                xy[a] = self.places[a, d]
                self.hops[a, d] = {"dp": (xy[0] * self.side + xy[1]) * 2 + self.c}

    def hop(self, axis, by):
        return self.hops[axis, by]

    def at(self, axis, by):
        return self.places[axis, by]

    def greet(self):
        barrier = pltpu.get_barrier_semaphore()
        others = [self.partner] + [self.hop(a, d) for a in (0, 1) for d in (1, -1)]
        for other in others:
            pl.semaphore_signal(barrier, inc=1, device_id=other, device_id_type=MESH)
        pl.semaphore_wait(barrier, len(others))


class Sems:
    def __init__(self, send, recv):
        self.send, self.recv, self.used, self.started = send, recv, 0, []

    def copy(self, src, dst, to):
        k = self.used
        self.used += 1
        made = pltpu.make_async_remote_copy(
            src_ref=src, dst_ref=dst, send_sem=self.send.at[k], recv_sem=self.recv.at[k], device_id=to, device_id_type=MESH
        )
        self.started.append(made)
        return made

    def finish(self):
        for made in self.started:
            made.wait_send()


def order(axis, a, b):
    return (a, b) if axis == 0 else (b, a)


class Gather:
    def __init__(self, place, sems, view, own, axis, lanes):
        n, other = place.side, 1 - axis
        p, q = place.at(axis, 0), place.at(other, 0)

        def slab(q, half=None):
            run = pl.ds(0, n) if half is None else pl.ds(half * (n // 2), n // 2)
            return view(*order(axis, run, q), None)

        self.sent_a, self.fwd_a, self.sent_b, self.fwd_b, self.swap = [], [], [], [], []
        mine = slab(q)
        self.swap.append(sems.copy(mine, mine, place.partner))
        for half, (d, part) in enumerate(zip((1, -1), halves(lanes), strict=True)):
            self.sent_a.append(sems.copy(own, view(*order(axis, p, q), None), place.hop(axis, d)))
            got = view(*order(axis, place.at(axis, -d), q), part)
            self.fwd_a.append(sems.copy(got, got, place.hop(axis, d)))
            self.sent_b.append(sems.copy(mine, mine, place.hop(other, d)))
            got = slab(place.at(other, -d), half)
            self.fwd_b.append(sems.copy(got, got, place.hop(other, d)))
            whole = slab(place.at(other, -d))
            self.swap.append(sems.copy(whole, whole, place.partner))
            got = slab(place.at(other, -2 * d), half)
            self.swap.append(sems.copy(got, got, place.partner))

    def a1(self):
        for copy in self.sent_a:
            copy.start()

    def a2(self):
        for k in (0, 1):
            self.sent_a[k].wait_recv()
            self.fwd_a[k].start()

    def b1(self):
        for copy in self.fwd_a:
            copy.wait_recv()
        for copy in self.sent_b:
            copy.start()
        self.swap[0].start()

    def b2(self):
        for k in (0, 1):
            self.sent_b[k].wait_recv()
            self.fwd_b[k].start()
            self.swap[1 + 2 * k].start()

    def c1(self):
        for k in (0, 1):
            self.fwd_b[k].wait_recv()
            self.swap[2 + 2 * k].start()

    def end(self):
        for copy in self.swap:
            copy.wait_recv()


def down_split(drows):
    first = (drows // 8 + 1) // 2 * 8
    return ((0, first), (first, drows - first))


COPIES = 13


def gather_phases(place, send, recv, local, shards, outs, praw, blk, layers):
    wg, wu, wd = shards
    c = place.c
    sems = Sems(send, recv)
    half = wg.shape[-1] // 2
    rows = wg.shape[1]
    flows, copies = [], []
    x, y = place.xy
    raws = [sems.copy(w, praw.at[1, j], place.partner) for j, w in enumerate((wg, wu))]
    loads = [pltpu.make_async_copy(w, praw.at[0, j], local.at[4 * len(layers) + j]) for j, w in enumerate((wg, wu))]
    at_once = 2 * len(layers)

    def add(own, view, axis, lanes):
        copies.append(pltpu.make_async_copy(own, view(x, y, None), local.at[len(copies)]))
        flows.append(Gather(place, sems, view, own, axis, lanes))

    for k, l in enumerate(layers):
        for j, (lo, m) in enumerate(down_split(wd.shape[1])):
            def view(xs, ys, part, k=k, lo=lo, m=m):
                lanes = ALL if part is None else pl.ds(*part)
                return outs[2].at[k, xs, ys, c, pl.ds(lo, m), lanes]
            add(wd.at[l, pl.ds(lo, m)], view, j, wd.shape[-1])
    for k in range(len(layers)):
        for j in (0, 1):
            def view(xs, ys, part, k=k, j=j):
                lo, m = (0, half) if part is None else part
                return outs[j].at[k, xs, ys, :, pl.ds(pl.multiple_of(c * half + lo, 128), m)]
            add(blk.at[j, k], view, j, half)

    def p0():
        for copy in raws + loads:
            copy.start()
        for copy, flow in zip(copies[:at_once], flows[:at_once], strict=True):
            copy.start()
            flow.a1()

    def p1():
        for j in (0, 1):
            loads[j].wait()
            raws[j].wait_recv()
            for k, l in enumerate(layers):
                for cc in (0, 1):
                    @pl.when(c == cc)
                    def _(cc=cc, j=j, k=k, l=l):
                        cols = slice(cc * half, (cc + 1) * half)
                        both = (praw[0, j, l, :, cols].astype(F32), praw[1, j, l, :, cols].astype(F32))
                        blk[j, k] = jnp.concatenate(both if cc == 0 else both[::-1], axis=0).astype(BF16)
        for copy, flow in zip(copies[at_once:], flows[at_once:], strict=True):
            copy.start()
            flow.a1()

    def every(step):
        def run():
            for flow in flows:
                getattr(flow, step)()
        return run

    def b1():
        for copy in copies:
            copy.wait()
        every("b1")()

    def end():
        every("end")()
        sems.finish()

    return [p0, p1, every("a2"), b1, every("b2"), every("c1"), end]


def gather(n, layers, wg, wu, wd, cid):
    side = math.isqrt(n // 2)
    L, rows, F = wg.shape
    drows, D = wd.shape[1:]
    k = len(layers)
    count = 2 + 4 * k * COPIES

    def kernel(wg, wu, wd, og, ou, od, praw, blk, send, recv, local):
        place = Place(n)
        place.greet()
        for phase in gather_phases(place, send, recv, local, (wg, wu, wd), (og, ou, od), praw, blk, layers):
            phase()

    out = pl.pallas_call(
        kernel,
        out_shape=[jax.ShapeDtypeStruct((k, side, side, 2 * rows, F), BF16)] * 2
        + [jax.ShapeDtypeStruct((k, side, side, 2, drows, D), BF16)],
        in_specs=[pl.BlockSpec(memory_space=pltpu.HBM)] * 3,
        out_specs=[pl.BlockSpec(memory_space=pltpu.HBM)] * 3,
        scratch_shapes=[
            pltpu.VMEM((2, 2, L, rows, F), BF16),
            pltpu.VMEM((2, k, 2 * rows, F // 2), BF16),
            pltpu.SemaphoreType.DMA((count,)),
            pltpu.SemaphoreType.DMA((count,)),
            pltpu.SemaphoreType.DMA((4 * k + 2,)),
        ],
        compiler_params=pltpu.CompilerParams(collective_id=cid, has_side_effects=True, vmem_limit_bytes=60 << 20),
        name=f"gather{cid}",
    )(wg, wu, wd)
    return [t.reshape(k, n * rows, F) for t in out[:2]] + [out[2].reshape(k, n * drows, D)]


class Scatter:
    def __init__(self, place, sems, axis, own, l1, part_a, full_a, total, snd_b, part_b, full_b):
        self.place, self.sems, self.axis = place, sems, axis
        self.own, self.l1, self.part_a, self.full_a, self.total, self.snd_b, self.part_b, self.full_b = (
            own, l1, part_a, full_a, total, snd_b, part_b, full_b)
        self.w = own.shape[-1]
        n, other = place.side, 1 - axis
        far_a, far_b = place.at(axis, 2), place.at(other, 2)
        self.sent_a, self.fwd_a, self.sent_b, self.fwd_b = [], [], [], []
        for h, (d, part) in enumerate(zip((1, -1), halves(self.w), strict=True)):
            run = pl.ds(h * (n // 2), n // 2)
            self.sent_a.append(sems.copy(own.at[order(axis, far_a, run)], part_a.at[h], place.hop(axis, d)))
            to = place.at(axis, d)
            self.fwd_a.append(sems.copy(own.at[order(axis, to, pl.ds(0, n))], full_a.at[h], place.hop(axis, d)))
            lanes = pl.ds(*part)
            self.sent_b.append(sems.copy(snd_b.at[far_b, :, lanes], part_b.at[h, :, lanes], place.hop(other, d)))
            self.fwd_b.append(sems.copy(snd_b.at[place.at(other, d)], full_b.at[h], place.hop(other, d)))

    def idx(self, a, b):
        return order(self.axis, a, b)

    def pair(self, a, b):
        i = self.idx(a, b)
        return self.own[i].astype(F32) + self.l1[i].astype(F32)

    def loop(self, lo, n, body):
        lax.fori_loop(lo, lo + n, lambda j, _: (body(j), 0)[1], 0)

    def a1(self):
        n = self.place.side
        far = self.place.at(self.axis, 2)

        def body(j):
            self.own[self.idx(far, j)] = self.pair(far, j).astype(BF16)

        self.loop(0, n, body)
        for copy in self.sent_a:
            copy.start()

    def a2(self):
        n = self.place.side
        for h, d in enumerate((1, -1)):
            to = self.place.at(self.axis, d)
            lo, rest = h * (n // 2), (1 - h) * (n // 2)

            def plain(j, to=to):
                self.own[self.idx(to, j)] = self.pair(to, j).astype(BF16)

            self.loop(rest, n // 2, plain)
            self.sent_a[h].wait_recv()

            def added(j, to=to, h=h, lo=lo):
                self.own[self.idx(to, j)] = (self.pair(to, j) + self.part_a[h, j - lo].astype(F32)).astype(BF16)

            self.loop(lo, n // 2, added)
            self.fwd_a[h].start()

    def b1(self):
        n = self.place.side
        p = self.place.at(self.axis, 0)
        for copy in self.fwd_a:
            copy.wait_recv()

        def body(j):
            self.total[j] = self.pair(p, j) + self.full_a[0, j].astype(F32) + self.full_a[1, j].astype(F32)

        self.loop(0, n, body)
        far = self.place.at(1 - self.axis, 2)
        self.snd_b[far] = self.total[far].astype(BF16)
        for copy in self.sent_b:
            copy.start()

    def b2(self):
        for h, (d, part) in enumerate(zip((1, -1), halves(self.w), strict=True)):
            to = self.place.at(1 - self.axis, d)
            lo, w = part
            rest = slice(w, self.w) if lo == 0 else slice(0, lo)
            got = slice(lo, lo + w)
            self.snd_b[to, :, rest] = self.total[to, :, rest].astype(BF16)
            self.sent_b[h].wait_recv()
            self.snd_b[to, :, got] = (self.total[to, :, got] + self.part_b[h, :, got].astype(F32)).astype(BF16)
            self.fwd_b[h].start()

    def last(self):
        for copy in self.fwd_b:
            copy.wait_recv()
        return self.total[self.place.at(1 - self.axis, 0)] + self.full_b[0].astype(F32) + self.full_b[1].astype(F32)


def scatter_scratch(side, r, w):
    return [
        pltpu.VMEM((side, side, r, w), BF16),
        pltpu.VMEM((side, side, r, w), BF16),
        pltpu.VMEM((2, side // 2, r, w), BF16),
        pltpu.VMEM((2, side, r, w), BF16),
        pltpu.VMEM((side, r, w), F32),
        pltpu.VMEM((side, r, w), BF16),
        pltpu.VMEM((2, r, w), BF16),
        pltpu.VMEM((2, r, w), BF16),
    ]


def scatter_phases(place, send, recv, local, terms, outs, swap, bufs):
    c = place.c
    sems = Sems(send, recv)
    half = terms[0].shape[-1] // 2
    drows = terms[2].shape[3]
    (lo0, n0), (lo1, n1) = down_split(drows)

    def cols(j, who):
        return terms[j].at[:, :, :, pl.ds(pl.multiple_of(who * half, 128), half)]

    def share(who):
        return [
            terms[2].at[:, :, who, pl.ds(lo0, n0), :],
            terms[2].at[:, :, who, pl.ds(lo1, n1), :],
            cols(0, who),
            cols(1, who),
        ]

    axes = (0, 1, 0, 1)
    flows = [Scatter(place, sems, axis, *buf) for axis, buf in zip(axes, bufs, strict=True)]
    first = [sems.copy(theirs, flow.l1, place.partner) for theirs, flow in zip(share(1 - c), flows, strict=True)]
    loads = [pltpu.make_async_copy(mine, flow.own, local.at[k]) for k, (mine, flow) in enumerate(zip(share(c), flows, strict=True))]
    swaps = [sems.copy(swap.at[0, j], swap.at[1, j], place.partner) for j in (0, 1)]

    def p0():
        for copy in first + loads:
            copy.start()

    def a1():
        for flow, got, load in zip(flows, first, loads, strict=True):
            load.wait()
            got.wait_recv()
            flow.a1()

    def every(step):
        def run():
            for flow in flows:
                getattr(flow, step)()
        return run

    def end():
        rows = outs[0].shape[0]
        outs[2][pl.ds(lo0, n0), :] = flows[0].last().astype(BF16)
        outs[2][pl.ds(lo1, n1), :] = flows[1].last().astype(BF16)
        for j in (0, 1):
            block = flows[2 + j].last()
            parts = (block[:rows].astype(BF16), block[rows:].astype(BF16))
            for cc in (0, 1):
                @pl.when(c == cc)
                def _(cc=cc, parts=parts, j=j):
                    outs[j][:, cc * half : (cc + 1) * half] = parts[cc]
                    swap[0, j] = parts[1 - cc]
            swaps[j].start()
        for j, copy in enumerate(swaps):
            copy.wait_recv()
            for cc in (0, 1):
                @pl.when(c == cc)
                def _(cc=cc, j=j):
                    outs[j][:, (1 - cc) * half : (2 - cc) * half] = swap[1, j]
        sems.finish()

    return [p0, a1, every("a2"), every("b1"), every("b2"), end]


def scatter_parts(n, dwg, dwu, dwd):
    side = math.isqrt(n // 2)
    D, F = dwg.shape
    rows, drows = D // n, F // n
    (_, n0), (_, n1) = down_split(drows)
    shapes = [(n0, D), (n1, D), (2 * rows, F // 2), (2 * rows, F // 2)]
    groups = [scatter_scratch(side, r, w) for r, w in shapes]
    count = 4 * 9 + 2
    operands = [dwg.reshape(side, side, 2 * rows, F), dwu.reshape(side, side, 2 * rows, F), dwd.reshape(side, side, 2, drows, D)]
    outs = [jax.ShapeDtypeStruct((rows, F), BF16)] * 2 + [jax.ShapeDtypeStruct((drows, D), BF16)]
    scratch = [
        pltpu.VMEM((2, 2, rows, F // 2), BF16),
        pltpu.SemaphoreType.DMA((count,)),
        pltpu.SemaphoreType.DMA((count,)),
        pltpu.SemaphoreType.DMA((4,)),
    ] + [s for group in groups for s in group]
    return operands, outs, [pl.BlockSpec(memory_space=pltpu.VMEM)] * 3, scratch, len(groups[0])


def scatter(n, dwg, dwu, dwd, cid):
    operands, outs, out_specs, scratch, each = scatter_parts(n, dwg, dwu, dwd)

    def kernel(dwg, dwu, dwd, og, ou, od, swap, send, recv, local, *flat):
        place = Place(n)
        place.greet()
        bufs = [flat[i * each : (i + 1) * each] for i in range(4)]
        for phase in scatter_phases(place, send, recv, local, (dwg, dwu, dwd), (og, ou, od), swap, bufs):
            phase()

    return pl.pallas_call(
        kernel,
        out_shape=outs,
        in_specs=[pl.BlockSpec(memory_space=pltpu.HBM)] * 3,
        out_specs=out_specs,
        scratch_shapes=scratch,
        compiler_params=pltpu.CompilerParams(collective_id=cid, has_side_effects=True, vmem_limit_bytes=60 << 20),
        name=f"scatter{cid}",
    )(*operands)


def dot(a, b, dims=((1,), (0,))):
    return lax.dot_general(a, b, (dims, ((), ())), preferred_element_type=F32)


ROWS_ROWS, COLS_COLS = ((0,), (0,)), ((1,), (1,))


def sigmoid(t):
    return 0.5 * jnp.tanh(0.5 * t) + 0.5


def scale_of(wide):
    return lax.rsqrt(jnp.mean(wide * wide, -1, keepdims=True) + 1e-6)


def normed(h):
    wide = h.astype(F32)
    return (wide * scale_of(wide)).astype(BF16)


def cut(n, most):
    return max(c for c in range(256, most + 1, 256) if n % c == 0)


def at_steps(phases, steps, step):
    for phase, k in zip(phases, steps, strict=True):
        pl.when(step == k)(phase)


HBM = pl.BlockSpec(memory_space=pltpu.HBM)
LIMIT = 62 << 20


def once(shape, index):
    return pl.BlockSpec(shape, index, pipeline_mode=pl.Buffered(1))


def forward(n, h, wg, wu, wd, shards, layer, cid):
    S, D = h.shape
    F = wg.shape[1]
    T, C = cut(S, 512), cut(F, 768)
    nt, nc = S // T, F // C
    side = math.isqrt(n // 2)
    L, rows, _ = shards[0].shape
    drows = shards[2].shape[1]
    count = 2 + 4 * COPIES
    steps = nt * nc
    when = [0, 1, 3, 5, steps - 2, steps, steps]

    def kernel(h, wg, wu, wd, sg, su, sd, o, og, ou, od, a, acc, praw, blk, send, recv, local):
        j = pl.program_id(1)
        step = pl.program_id(0) * nc + j
        place = Place(n)
        pl.when(step == 0)(place.greet)
        phases = gather_phases(place, send, recv, local, (sg, su, sd), (og, ou, od), praw, blk, (layer,))
        for phase, k in zip(phases, when, strict=True):
            if k < steps:
                pl.when(step == k)(phase)

        @pl.when(j == 0)
        def _():
            a[...] = normed(h[...])
            acc[...] = jnp.zeros_like(acc)

        gate, up = dot(a[...], wg[...]), dot(a[...], wu[...])
        act = (gate * sigmoid(gate) * up).astype(BF16)
        acc[...] += dot(act, wd[...])

        @pl.when(j == nc - 1)
        def _():
            o[...] = (h[...].astype(F32) + acc[...].astype(BF16).astype(F32)).astype(BF16)

        @pl.when(step == steps - 1)
        def _():
            for phase, k in zip(phases, when, strict=True):
                if k >= steps:
                    phase()

    flops = 6 * S * D * F
    out = pl.pallas_call(
        kernel,
        grid=(nt, nc),
        out_shape=[jax.ShapeDtypeStruct((S, D), BF16)]
        + [jax.ShapeDtypeStruct((1, side, side, 2 * rows, F), BF16)] * 2
        + [jax.ShapeDtypeStruct((1, side, side, 2, drows, D), BF16)],
        in_specs=[
            pl.BlockSpec((T, D), lambda i, j: (i, 0)),
            pl.BlockSpec((D, C), lambda i, j: (0, j)),
            pl.BlockSpec((D, C), lambda i, j: (0, j)),
            pl.BlockSpec((C, D), lambda i, j: (j, 0)),
            HBM,
            HBM,
            HBM,
        ],
        out_specs=[pl.BlockSpec((T, D), lambda i, j: (i, 0)), HBM, HBM, HBM],
        scratch_shapes=[
            pltpu.VMEM((T, D), BF16),
            pltpu.VMEM((T, D), F32),
            pltpu.VMEM((2, 2, L, rows, F), BF16),
            pltpu.VMEM((2, 1, 2 * rows, F // 2), BF16),
            pltpu.SemaphoreType.DMA((count,)),
            pltpu.SemaphoreType.DMA((count,)),
            pltpu.SemaphoreType.DMA((6,)),
        ],
        compiler_params=pltpu.CompilerParams(
            collective_id=cid, has_side_effects=True, vmem_limit_bytes=LIMIT, dimension_semantics=("arbitrary", "arbitrary")
        ),
        cost_estimate=pl.CostEstimate(flops=flops, bytes_accessed=4 * S * D, transcendentals=S * F),
        name="forward",
    )(h, wg, wu, wd, *shards)
    return out[0], (out[1].reshape(n * rows, F), out[2].reshape(n * rows, F), out[3].reshape(n * drows, D))


def backward(n, h, dy, wg, wu, wd, terms, cid):
    S, D = h.shape
    F = wg.shape[1]
    T, C = cut(S, 512), cut(F, 768)
    nt, nc = S // T, F // C
    steps = nt * nc
    when = [0, 2, 5, 9, 10, steps]
    if terms is None:
        more_in, more_out, more_specs, scratch, kind = [], [], [], [], {}
    else:
        more_in, more_out, more_specs, scratch, each = scatter_parts(n, *terms)
        kind = {"collective_id": cid, "has_side_effects": True}

    def kernel(h, dy, wg, wu, wd, *rest):
        terms_, rest = rest[: len(more_in)], rest[len(more_in) :]
        (act, dg, du, a, dh), rest = rest[:5], rest[5:]
        outs, rest = rest[: len(more_out)], rest[len(more_out) :]
        acc, rest = rest[0], rest[1:]
        j = pl.program_id(1)
        step = pl.program_id(0) * nc + j
        if terms is not None:
            place = Place(n)
            pl.when(step == 0)(place.greet)
            swap, send, recv, local, *flat = rest
            bufs = [flat[i * each : (i + 1) * each] for i in range(4)]
            phases = scatter_phases(place, send, recv, local, terms_, outs, swap, bufs)
            for phase, k in zip(phases, when, strict=True):
                if k < steps:
                    pl.when(step == k)(phase)

        @pl.when(j == 0)
        def _():
            a[...] = normed(h[...])
            acc[...] = jnp.zeros_like(acc)

        gate, up = dot(a[...], wg[...]), dot(a[...], wu[...])
        dact = dot(dy[...], wd[...], COLS_COLS).astype(BF16).astype(F32)
        sig = sigmoid(gate)
        silu = gate * sig
        act[...] = (silu * up).astype(BF16)
        by_up = (dact * silu).astype(BF16)
        by_gate = (dact * up * (sig + silu * (1.0 - sig))).astype(BF16)
        du[...] = by_up
        dg[...] = by_gate
        acc[...] += dot(by_gate, wg[...], COLS_COLS) + dot(by_up, wu[...], COLS_COLS)

        @pl.when(j == nc - 1)
        def _():
            by_a = acc[...].astype(BF16).astype(F32)
            wide = h[...].astype(F32)
            scale = scale_of(wide)
            hat = wide * scale
            by_wide = scale * (by_a - hat * jnp.mean(by_a * hat, -1, keepdims=True))
            dh[...] = (dy[...].astype(F32) + by_wide.astype(BF16).astype(F32)).astype(BF16)

        if terms is not None:
            @pl.when(step == steps - 1)
            def _():
                for phase, k in zip(phases, when, strict=True):
                    if k >= steps:
                        phase()

    tile = pl.BlockSpec((T, D), lambda i, j: (i, 0))
    wide_tile = pl.BlockSpec((T, C), lambda i, j: (i, j))
    out = pl.pallas_call(
        kernel,
        grid=(nt, nc),
        out_shape=[jax.ShapeDtypeStruct((S, F), BF16)] * 3 + [jax.ShapeDtypeStruct((S, D), BF16)] * 2 + more_out,
        in_specs=[
            tile,
            tile,
            pl.BlockSpec((D, C), lambda i, j: (0, j)),
            pl.BlockSpec((D, C), lambda i, j: (0, j)),
            pl.BlockSpec((C, D), lambda i, j: (j, 0)),
        ]
        + [HBM] * len(more_in),
        out_specs=[wide_tile] * 3 + [tile] * 2 + more_specs,
        scratch_shapes=[pltpu.VMEM((T, D), F32)] + scratch,
        compiler_params=pltpu.CompilerParams(vmem_limit_bytes=LIMIT, dimension_semantics=("arbitrary", "arbitrary"), **kind),
        cost_estimate=pl.CostEstimate(flops=10 * S * D * F, bytes_accessed=6 * S * F, transcendentals=S * F),
        name=f"backward{cid}",
    )(h, dy, wg, wu, wd, *more_in)
    return out[:5], out[5:]


def weights_kernel(a, dy, act, dg, du):
    S, D = a.shape
    F = act.shape[1]
    C = cut(F, 768)
    nc = F // C

    def kernel(a, dy, act, dg, du, og, ou, od):
        step = pl.program_id(0)

        @pl.when(step < nc)
        def _():
            od[...] = dot(act[...], dy[...], ROWS_ROWS).astype(BF16)

        @pl.when((step >= nc) & (step < 2 * nc))
        def _():
            og[...] = dot(a[...], dg[...], ROWS_ROWS).astype(BF16)

        @pl.when(step >= 2 * nc)
        def _():
            ou[...] = dot(a[...], du[...], ROWS_ROWS).astype(BF16)

    def at(k):
        return lambda i: jnp.clip(i - k * nc, 0, nc - 1)

    def cols(k, rows):
        f = at(k)
        return pl.BlockSpec((rows, C), lambda i: (0, f(i)))

    down = at(0)
    return pl.pallas_call(
        kernel,
        grid=(3 * nc,),
        out_shape=[jax.ShapeDtypeStruct((D, F), BF16)] * 2 + [jax.ShapeDtypeStruct((F, D), BF16)],
        in_specs=[once((S, D), lambda i: (0, 0))] * 2 + [cols(0, S), cols(1, S), cols(2, S)],
        out_specs=[cols(1, D), cols(2, D), pl.BlockSpec((C, D), lambda i: (down(i), 0))],
        compiler_params=pltpu.CompilerParams(vmem_limit_bytes=LIMIT, dimension_semantics=("arbitrary",)),
        cost_estimate=pl.CostEstimate(flops=6 * S * D * F, bytes_accessed=6 * S * F, transcendentals=0),
        name="weights",
    )(a, dy, act, dg, du)


def solution(mesh):
    n = mesh.shape["dp"]

    def device(x, dy, wg, wu, wd):
        shards = (wg, wu, wd)
        layers = wg.shape[0]
        x, dy = x.reshape(x.shape[1:]), dy.reshape(dy.shape[1:])
        states, weights = [x], [tuple(t[0] for t in gather(n, (0,), *shards, 0))]
        for l in range(layers - 1):
            h, more = forward(n, states[l], *weights[l], shards, l + 1, 1 + l)
            states.append(h)
            weights.append(more)
        terms, sums = None, []
        for l in reversed(range(layers)):
            (act, dg, du, a, dh), done = backward(n, states[l], dy, *weights[l], terms, layers + 1 + l)
            if terms is not None:
                sums.append(done)
            terms = weights_kernel(a, dy, act, dg, du)
            dy = dh
        sums.append(scatter(n, *terms, 2 * layers + 1))
        return (dy[None], *(jnp.stack([s[j] for s in sums[::-1]]) for j in range(3)))

    tokens, rows = P(("rep", "dp")), P(None, "dp")
    return jax.shard_map(
        device, mesh=mesh, in_specs=(tokens, tokens, rows, rows, rows), out_specs=(tokens, *[P("rep", "dp")] * 3), check_vma=False
    )
```

time: 522 us -> 379 us (0.73)
  matrix products: 286 us -> 0 us
  Pallas kernels: 173 us -> 367 us
  local copies, waits for them, and re-layouts: 43.2 us -> 7.16 us
  other arithmetic: 14 us -> 3.52 us
    dot_general x17 -> x0, matrix products: 286 us -> none  [dot(): return lax.dot_general(a, b, (dims, ((), ())), preferred_element_type=F32)]
    pallas_call x2 -> x6, Pallas kernels: 94.1 us -> 320 us  [the longest x2 146 us: backward(): pl.pallas_call(kernel, grid=(nt, nc), out_shape=[jax.ShapeDtypeStruct((S,...]
    pallas_call x1, Pallas kernels: 79.1 us -> 47.2 us  [gather(): pl.pallas_call(kernel, out_shape=[jax.ShapeDtypeStruct((k, side, side, 2...]
    unnamed x53 -> x13, local copies, waits for them, and re-layouts: 29.2 us -> 7.16 us
    slice x2 -> x0, local copies, waits for them, and re-layouts: 14 us -> none  [device(): weights = [(gg[l], gu[l], gd[l]) for l in layers]]
where the time goes in v2:
time: 379 us
  Pallas kernels  367 us (97%)
  local copies, waits for them, and re-layouts  7.16 us (2%)
    pallas_call x2, Pallas kernels, backward(): pl.pallas_call(kernel, grid=(nt, nc), out_shape=[jax.ShapeDtypeStruct((S,...  146 us
    pallas_call x2, Pallas kernels, weights_kernel(): pl.pallas_call(kernel, grid=(3 * nc,), out_shape=[jax.ShapeDtypeStruct((D...  75 us
    pallas_call x1, Pallas kernels, forward(): pl.pallas_call(kernel, grid=(nt, nc), out_shape=[jax.ShapeDtypeStruct((S,...  52.3 us
    pallas_call x1, Pallas kernels, gather(): pl.pallas_call(kernel, out_shape=[jax.ShapeDtypeStruct((k, side, side, 2...  47.2 us
    pallas_call x1, Pallas kernels, scatter(): pl.pallas_call(kernel, out_shape=outs, in_specs=[pl.BlockSpec(memory_spac...  46.6 us

profile of v2, /device:TPU:97, one launch (start us, length us, event | category | flops | bytes accessed | tf_op | source)
XLA Modules:
  0.0 378.7 jit_solution(7062056640367265621)
XLA Ops:
  0.6 1.7 copy.9.wg.sg
  2.3 1.7 copy.10.wu.su
  4.0 47.2 %gather0.1 = (bf16[1,4,4,56,2304]{4,3,2,1,0:T(8,128)(2,1)}, bf16[1,4,4,56,2304]{4,3,2,1,0:T(8,128)(2,1)}, bf16[1,4,4,2,72,896]{5,4,3,2,1,0:T(8,128)(2,1)}) custom-call(bf16[2,28,2304]{2,1,0:T(8,128)(2,1)} %copy.9.wg.sg, bf16[2,28,2304]{2,1,0:T(8,128)(2,1)} %copy.10.wu.su, bf16[2,72,896]{2,1,0:T(8,128)(2,1)} %sd.1), custom_call_target="tpu_custom_call" | custom-call | tf_op jit(solution)/shard_map/gather0/pallas_call | solution.py:218
  51.2 52.3 %forward.1 = (bf16[2048,896]{1,0:T(8,128)(2,1)}, bf16[1,4,4,56,2304]{4,3,2,1,0:T(8,128)(2,1)}, bf16[1,4,4,56,2304]{4,3,2,1,0:T(8,128)(2,1)}, bf16[1,4,4,2,72,896]{5,4,3,2,1,0:T(8,128)(2,1)}) custom-call(bf16[2048,896]{1,0:T(8,128)(2,1)} %bitcast.39, bf16[896,2304]{1,0:T(8,128)(2,1)} %bitcast.31, bf16[896,2304]{1,0:T(8,128)(2,1)} %bitcast.33, ...), custom_call_target="tpu_custom_call" | custom-call | flops 25367150592 | bytes 7340032 | tf_op jit(solution)/shard_map/forward/pallas_call | solution.py:522
  103.5 67.4 %backward4.1 = (bf16[2048,2304]{1,0:T(8,128)(2,1)}, bf16[2048,2304]{1,0:T(8,128)(2,1)}, bf16[2048,2304]{1,0:T(8,128)(2,1)}, bf16[2048,896]{1,0:T(8,128)(2,1)}, bf16[2048,896]{1,0:T(8,128)(2,1)}) custom-call(bf16[2048,896]{1,0:T(8,128)(2,1)} %get-tuple-element.36.h, bf16[2048,896]{1,0:T(8,128)(2,1)} %bitcast.37, bf16[896,2304]{1,0:T(8,128)(2,1)} %bitcast.44, ...), custom_call_target="tpu_custom_call" | custom-call | flops 42278584320 | bytes 28311552 | tf_op jit(solution)/shard_map/backward4/pallas_call | solution.py:620
  170.9 37.4 %weights.2 = (bf16[896,2304]{1,0:T(8,128)(2,1)}, bf16[896,2304]{1,0:T(8,128)(2,1)}, bf16[2304,896]{1,0:T(8,128)(2,1)}) custom-call(bf16[2048,896]{1,0:T(8,128)(2,1)} %get-tuple-element.41.a, bf16[2048,896]{1,0:T(8,128)(2,1)} %bitcast.38, bf16[2048,2304]{1,0:T(8,128)(2,1)} %get-tuple-element.42.act, bf16[2048,2304]{1,0:T(8,128)(2,1)} %get-tuple-element.43.dg, ...), custom_call_target="tpu_custom_call" | custom-call | flops 25367150592 | bytes 28311552 | tf_op jit(solution)/shard_map/weights/pallas_call | solution.py:670
  208.4 78.9 %backward3.1 = (bf16[2048,2304]{1,0:T(8,128)(2,1)}, bf16[2048,2304]{1,0:T(8,128)(2,1)}, bf16[2048,2304]{1,0:T(8,128)(2,1)}, bf16[2048,896]{1,0:T(8,128)(2,1)}, b...) custom-call(bf16[2048,896]{1,0:T(8,128)(2,1)} %bitcast.40, ...), custom_call_target="tpu_custom_call" | custom-call | flops 42278584320 | bytes 28311552 | tf_op jit(solution)/shard_map/backward3/pallas_call | solution.py:620
  287.2 37.6 %weights.3 = (bf16[896,2304]{1,0:T(8,128)(2,1)}, bf16[896,2304]{1,0:T(8,128)(2,1)}, bf16[2304,896]{1,0:T(8,128)(2,1)}) custom-call(bf16[2048,896]{1,0:T(8,128)(2,1)} %get-tuple-element.49.a, bf16[2048,896]{1,0:T(8,128)(2,1)} %get-tuple-element.40.dy, bf16[2048,2304]{1,0:T(8,128)(2,1)} %get-tuple-element.50.act, bf16[2048,2304]{1,0:T(8,128)(2,1)} %get-tuple-element.51.dg, ...), custom_call_target="tpu_custom_call" | custom-call | flops 25367150592 | bytes 28311552 | tf_op jit(solution)/shard_map/weights/pallas_call | solution.py:670
  324.8 0.0 copy-start.2
  324.8 0.0 copy-start.1
  324.8 0.0 copy-start.3
  324.8 0.0 copy-start
  324.8 46.6 %scatter5.1 = (bf16[28,2304]{1,0:T(8,128)(2,1)}, bf16[28,2304]{1,0:T(8,128)(2,1)}, bf16[72,896]{1,0:T(8,128)(2,1)}) custom-call(bf16[4,4,56,2304]{3,2,1,0:T(8,128)(2,1)} %bitcast.21, bf16[4,4,56,2304]{3,2,1,0:T(8,128)(2,1)} %bitcast.22, bf16[4,4,2,72,896]{4,3,2,1,0:T(8,128)(2,1)} %bitcast.23), custom_call_target="tpu_custom_call" | custom-call | tf_op jit(solution)/shard_map/scatter5/pallas_call | solution.py:432
  371.3 0.0 copy-done.2
  371.4 0.9 pad_maximum_fusion
  372.3 1.0 copy.13
  373.3 0.0 copy-done.1
  373.3 0.9 pad_maximum_fusion.1
  374.2 1.0 copy.14
  375.2 0.0 copy-done.3
  375.2 1.6 pad_maximum_fusion.2
  376.8 0.0 copy-done
  376.8 1.8 copy.16
Async XLA Ops:
  324.8 46.6 %copy-start.2 = (bf16[28,2304]{1,0:T(8,128)(2,1)S(1)}, bf16[28,2304]{1,0:T(8,128)(2,1)}, u32[]{:S(2)}) copy-start(bf16[28,2304]{1,0:T(8,128)(2,1)} %get-tuple-element.57) | copy-start | bytes 387076
  324.8 48.5 %copy-start.1 = (bf16[28,2304]{1,0:T(8,128)(2,1)S(1)}, bf16[28,2304]{1,0:T(8,128)(2,1)}, u32[]{:S(2)}) copy-start(bf16[28,2304]{1,0:T(8,128)(2,1)} %get-tuple-element.59) | copy-start | bytes 387076
  324.8 50.4 %copy-start.3 = (bf16[72,896]{1,0:T(8,128)(2,1)S(1)}, bf16[72,896]{1,0:T(8,128)(2,1)}, u32[]{:S(2)}) copy-start(bf16[72,896]{1,0:T(8,128)(2,1)} %get-tuple-element.61) | copy-start | bytes 387076
  324.8 52.0 %copy-start = (bf16[2048,896]{1,0:T(8,128)(2,1)S(1)}, bf16[2048,896]{1,0:T(8,128)(2,1)}, u32[]{:S(2)}) copy-start(bf16[2048,896]{1,0:T(8,128)(2,1)} %get-tuple-element.48) | copy-start | bytes 11010052

commit v3 on v2

v3 whole, which is shorter than its diff:
```python
import functools
import math
import jax
import jax.numpy as jnp
from jax import lax
from jax.experimental import pallas as pl
from jax.experimental.pallas import tpu as pltpu
from jax.sharding import PartitionSpec as P

MESH = pl.DeviceIdType.MESH
F32, BF16 = jnp.float32, jnp.bfloat16
ALL = slice(None)


def halves(n):
    first = (n // 128 + 1) // 2 * 128
    return (0, first), (first, n - first)


class Place:
    def __init__(self, n):
        self.side = math.isqrt(n // 2)
        me = lax.axis_index("dp")
        chip = me // 2
        self.c = me % 2
        self.xy = (chip // self.side, chip % self.side)
        self.partner = {"dp": chip * 2 + 1 - self.c}
        self.places = {(a, d): lax.rem(self.xy[a] + d + self.side, self.side) for a in (0, 1) for d in range(-2, 3)}
        self.hops = {}
        for a in (0, 1):
            for d in (1, -1):
                xy = list(self.xy)
                xy[a] = self.places[a, d]
                self.hops[a, d] = {"dp": (xy[0] * self.side + xy[1]) * 2 + self.c}

    def hop(self, axis, by):
        return self.hops[axis, by]

    def at(self, axis, by):
        return self.places[axis, by]

    def greet(self):
        barrier = pltpu.get_barrier_semaphore()
        others = [self.partner] + [self.hop(a, d) for a in (0, 1) for d in (1, -1)]
        for other in others:
            pl.semaphore_signal(barrier, inc=1, device_id=other, device_id_type=MESH)
        pl.semaphore_wait(barrier, len(others))


class Sems:
    def __init__(self, send, recv):
        self.send, self.recv, self.used, self.started = send, recv, 0, []

    def copy(self, src, dst, to):
        k = self.used
        self.used += 1
        made = pltpu.make_async_remote_copy(
            src_ref=src, dst_ref=dst, send_sem=self.send.at[k], recv_sem=self.recv.at[k], device_id=to, device_id_type=MESH
        )
        self.started.append(made)
        return made

    def finish(self):
        for made in self.started:
            made.wait_send()


def order(axis, a, b):
    return (a, b) if axis == 0 else (b, a)


class Gather:
    def __init__(self, place, sems, view, own, axis, lanes):
        n, other = place.side, 1 - axis
        p, q = place.at(axis, 0), place.at(other, 0)

        def slab(q, half=None):
            run = pl.ds(0, n) if half is None else pl.ds(half * (n // 2), n // 2)
            return view(*order(axis, run, q), None)

        self.sent_a, self.fwd_a, self.sent_b, self.fwd_b, self.swap = [], [], [], [], []
        mine = slab(q)
        self.swap.append(sems.copy(mine, mine, place.partner))
        for half, (d, part) in enumerate(zip((1, -1), halves(lanes), strict=True)):
            self.sent_a.append(sems.copy(own, view(*order(axis, p, q), None), place.hop(axis, d)))
            got = view(*order(axis, place.at(axis, -d), q), part)
            self.fwd_a.append(sems.copy(got, got, place.hop(axis, d)))
            self.sent_b.append(sems.copy(mine, mine, place.hop(other, d)))
            got = slab(place.at(other, -d), half)
            self.fwd_b.append(sems.copy(got, got, place.hop(other, d)))
            whole = slab(place.at(other, -d))
            self.swap.append(sems.copy(whole, whole, place.partner))
            got = slab(place.at(other, -2 * d), half)
            self.swap.append(sems.copy(got, got, place.partner))

    def a1(self):
        for copy in self.sent_a:
            copy.start()

    def a2(self):
        for k in (0, 1):
            self.sent_a[k].wait_recv()
            self.fwd_a[k].start()

    def b1(self):
        for copy in self.fwd_a:
            copy.wait_recv()
        for copy in self.sent_b:
            copy.start()
        self.swap[0].start()

    def b2(self):
        for k in (0, 1):
            self.sent_b[k].wait_recv()
            self.fwd_b[k].start()
            self.swap[1 + 2 * k].start()

    def c1(self):
        for k in (0, 1):
            self.fwd_b[k].wait_recv()
            self.swap[2 + 2 * k].start()

    def end(self):
        for copy in self.swap:
            copy.wait_recv()

    def got_a(self):
        for copy in self.fwd_a:
            copy.wait_recv()

    def b1_next(self):
        for copy in self.sent_b:
            copy.start()
        self.swap[0].start()

    def sends(self, first):
        for copy in self.sent_a + self.fwd_a if first else self.sent_b + self.fwd_b + self.swap:
            copy.wait_send()


def down_split(drows):
    first = (drows // 8 + 1) // 2 * 8
    return ((0, first), (first, drows - first))


COPIES = 13


def gather_flows(place, sems, outs, owns):
    c = place.c
    half = outs[0].shape[-1] // 2
    D = outs[2].shape[-1]
    flows, views = [], []
    for j, (lo, m) in enumerate(down_split(outs[2].shape[3])):
        def view(xs, ys, part, lo=lo, m=m):
            return outs[2].at[xs, ys, c, pl.ds(lo, m), ALL if part is None else pl.ds(*part)]
        views.append((view, j, D))
    for j in (0, 1):
        def view(xs, ys, part, j=j):
            lo, m = (0, half) if part is None else part
            return outs[j].at[xs, ys, :, pl.ds(pl.multiple_of(c * half + lo, 128), m)]
        views.append((view, j, half))
    mine = [view(*place.xy, None) for view, _, _ in views]
    flows = [Gather(place, sems, view, own, axis, lanes) for (view, axis, lanes), own in zip(views, owns or mine, strict=True)]
    return flows, mine


def gather_shapes(n, rows, F, drows, D):
    side = math.isqrt(n // 2)
    return [jax.ShapeDtypeStruct((side, side, 2 * rows, F), BF16)] * 2 + [jax.ShapeDtypeStruct((side, side, 2, drows, D), BF16)]


def whole(n, arrays):
    g, u, d = arrays
    return g.reshape(-1, g.shape[-1]), u.reshape(-1, u.shape[-1]), d.reshape(-1, d.shape[-1])


def gather(n, wg, wu, wd, cid):
    L, rows, F = wg.shape
    drows, D = wd.shape[1:]
    layers = 2
    half = F // 2
    count = 2 + 4 * layers * COPIES

    def kernel(wg, wu, wd, *rest):
        outs = rest[:3], rest[3:6]
        praw, blk, send, recv, local = rest[6:]
        place = Place(n)
        c = place.c
        place.greet()
        sems = Sems(send, recv)
        raws = [sems.copy(w, praw.at[1, j], place.partner) for j, w in enumerate((wg, wu))]
        loads = [pltpu.make_async_copy(w, praw.at[0, j], local.at[j]) for j, w in enumerate((wg, wu))]
        flows, copies = [], []
        for l in range(layers):
            owns = [wd.at[l, pl.ds(lo, m)] for lo, m in down_split(drows)] + [blk.at[j, l] for j in (0, 1)]
            some, mine = gather_flows(place, sems, outs[l], owns)
            flows.append(some)
            copies.append([pltpu.make_async_copy(o, m, local.at[2 + 4 * l + k]) for k, (o, m) in enumerate(zip(owns, mine, strict=True))])

        def each(l, step, picked=slice(None)):
            for flow in flows[l][picked]:
                getattr(flow, step)()

        for copy in raws + loads + copies[0][:2] + copies[1][:2]:
            copy.start()
        each(0, "a1", slice(0, 2))
        for j in (0, 1):
            loads[j].wait()
            raws[j].wait_recv()
            for l in range(layers):
                for cc in (0, 1):
                    @pl.when(c == cc)
                    def _(cc=cc, j=j, l=l):
                        cols = slice(cc * half, (cc + 1) * half)
                        both = (praw[0, j, l, :, cols].astype(F32), praw[1, j, l, :, cols].astype(F32))
                        blk[j, l] = jnp.concatenate(both if cc == 0 else both[::-1], axis=0).astype(BF16)
        for copy in copies[0][2:] + copies[1][2:]:
            copy.start()
        each(0, "a1", slice(2, 4))
        each(0, "a2")
        for copy in copies[0]:
            copy.wait()
        each(0, "b1")
        each(1, "a1")
        each(0, "b2")
        each(1, "a2")
        each(0, "c1")
        each(0, "end")
        each(1, "got_a")
        for copy in copies[1]:
            copy.wait()
        for copy in raws:
            copy.wait_send()
        for flow in flows[0]:
            flow.sends(True)
            flow.sends(False)
        for flow in flows[1]:
            flow.sends(True)

    out = pl.pallas_call(
        kernel,
        out_shape=gather_shapes(n, rows, F, drows, D) * layers,
        in_specs=[pl.BlockSpec(memory_space=pltpu.HBM)] * 3,
        out_specs=[pl.BlockSpec(memory_space=pltpu.HBM)] * 6,
        scratch_shapes=[
            pltpu.VMEM((2, 2, L, rows, F), BF16),
            pltpu.VMEM((2, layers, 2 * rows, half), BF16),
            pltpu.SemaphoreType.DMA((count,)),
            pltpu.SemaphoreType.DMA((count,)),
            pltpu.SemaphoreType.DMA((2 + 4 * layers,)),
        ],
        compiler_params=pltpu.CompilerParams(collective_id=cid, has_side_effects=True, vmem_limit_bytes=60 << 20),
        name="gather",
    )(wg, wu, wd)
    return out[:3], out[3:]


class Scatter:
    def __init__(self, place, sems, axis, own, l1, part_a, full_a, total, snd_b, part_b, full_b):
        self.place, self.sems, self.axis = place, sems, axis
        self.own, self.l1, self.part_a, self.full_a, self.total, self.snd_b, self.part_b, self.full_b = (
            own, l1, part_a, full_a, total, snd_b, part_b, full_b)
        self.w = own.shape[-1]
        n, other = place.side, 1 - axis
        far_a, far_b = place.at(axis, 2), place.at(other, 2)
        self.sent_a, self.fwd_a, self.sent_b, self.fwd_b = [], [], [], []
        for h, (d, part) in enumerate(zip((1, -1), halves(self.w), strict=True)):
            run = pl.ds(h * (n // 2), n // 2)
            self.sent_a.append(sems.copy(own.at[order(axis, far_a, run)], part_a.at[h], place.hop(axis, d)))
            to = place.at(axis, d)
            self.fwd_a.append(sems.copy(own.at[order(axis, to, pl.ds(0, n))], full_a.at[h], place.hop(axis, d)))
            lanes = pl.ds(*part)
            self.sent_b.append(sems.copy(snd_b.at[far_b, :, lanes], part_b.at[h, :, lanes], place.hop(other, d)))
            self.fwd_b.append(sems.copy(snd_b.at[place.at(other, d)], full_b.at[h], place.hop(other, d)))

    def idx(self, a, b):
        return order(self.axis, a, b)

    def pair(self, a, b):
        i = self.idx(a, b)
        return self.own[i].astype(F32) + self.l1[i].astype(F32)

    def loop(self, lo, n, body):
        lax.fori_loop(lo, lo + n, lambda j, _: (body(j), 0)[1], 0)

    def a1(self):
        n = self.place.side
        far = self.place.at(self.axis, 2)

        def body(j):
            self.own[self.idx(far, j)] = self.pair(far, j).astype(BF16)

        self.loop(0, n, body)
        for copy in self.sent_a:
            copy.start()

    def a2(self):
        n = self.place.side
        for h, d in enumerate((1, -1)):
            to = self.place.at(self.axis, d)
            lo, rest = h * (n // 2), (1 - h) * (n // 2)

            def plain(j, to=to):
                self.own[self.idx(to, j)] = self.pair(to, j).astype(BF16)

            self.loop(rest, n // 2, plain)
            self.sent_a[h].wait_recv()

            def added(j, to=to, h=h, lo=lo):
                self.own[self.idx(to, j)] = (self.pair(to, j) + self.part_a[h, j - lo].astype(F32)).astype(BF16)

            self.loop(lo, n // 2, added)
            self.fwd_a[h].start()

    def b1(self):
        n = self.place.side
        p = self.place.at(self.axis, 0)
        for copy in self.fwd_a:
            copy.wait_recv()

        def body(j):
            self.total[j] = self.pair(p, j) + self.full_a[0, j].astype(F32) + self.full_a[1, j].astype(F32)

        self.loop(0, n, body)
        far = self.place.at(1 - self.axis, 2)
        self.snd_b[far] = self.total[far].astype(BF16)
        for copy in self.sent_b:
            copy.start()

    def b2(self):
        for h, (d, part) in enumerate(zip((1, -1), halves(self.w), strict=True)):
            to = self.place.at(1 - self.axis, d)
            lo, w = part
            rest = slice(w, self.w) if lo == 0 else slice(0, lo)
            got = slice(lo, lo + w)
            self.snd_b[to, :, rest] = self.total[to, :, rest].astype(BF16)
            self.sent_b[h].wait_recv()
            self.snd_b[to, :, got] = (self.total[to, :, got] + self.part_b[h, :, got].astype(F32)).astype(BF16)
            self.fwd_b[h].start()

    def last(self):
        for copy in self.fwd_b:
            copy.wait_recv()
        return self.total[self.place.at(1 - self.axis, 0)] + self.full_b[0].astype(F32) + self.full_b[1].astype(F32)


def scatter_scratch(side, r, w):
    return [
        pltpu.VMEM((side, side, r, w), BF16),
        pltpu.VMEM((side, side, r, w), BF16),
        pltpu.VMEM((2, side // 2, r, w), BF16),
        pltpu.VMEM((2, side, r, w), BF16),
        pltpu.VMEM((side, r, w), F32),
        pltpu.VMEM((side, r, w), BF16),
        pltpu.VMEM((2, r, w), BF16),
        pltpu.VMEM((2, r, w), BF16),
    ]


def scatter_phases(place, send, recv, local, terms, outs, swap, bufs):
    c = place.c
    sems = Sems(send, recv)
    down = len(terms) == 1
    half = terms[0].shape[-1] // 2

    def share(who):
        if down:
            return [terms[0].at[:, :, who, pl.ds(lo, m), :] for lo, m in down_split(terms[0].shape[3])]
        lanes = pl.ds(pl.multiple_of(who * half, 128), half)
        return [term.at[:, :, :, lanes] for term in terms]

    flows = [Scatter(place, sems, axis, *buf) for axis, buf in enumerate(bufs)]
    first = [sems.copy(theirs, flow.l1, place.partner) for theirs, flow in zip(share(1 - c), flows, strict=True)]
    loads = [pltpu.make_async_copy(mine, flow.own, local.at[k]) for k, (mine, flow) in enumerate(zip(share(c), flows, strict=True))]
    swaps = [] if down else [sems.copy(swap.at[0, j], swap.at[1, j], place.partner) for j in (0, 1)]

    def p0():
        for copy in first + loads:
            copy.start()

    def a1():
        for flow, got, load in zip(flows, first, loads, strict=True):
            load.wait()
            got.wait_recv()
            flow.a1()

    def every(step):
        def run():
            for flow in flows:
                getattr(flow, step)()
        return run

    def end():
        if down:
            for (lo, m), flow in zip(down_split(terms[0].shape[3]), flows, strict=True):
                outs[0][pl.ds(lo, m), :] = flow.last().astype(BF16)
        else:
            rows = outs[0].shape[0]
            for j in (0, 1):
                block = flows[j].last()
                parts = (block[:rows].astype(BF16), block[rows:].astype(BF16))
                for cc in (0, 1):
                    @pl.when(c == cc)
                    def _(cc=cc, parts=parts, j=j):
                        outs[j][:, cc * half : (cc + 1) * half] = parts[cc]
                        swap[0, j] = parts[1 - cc]
                swaps[j].start()
            for j, copy in enumerate(swaps):
                copy.wait_recv()
                for cc in (0, 1):
                    @pl.when(c == cc)
                    def _(cc=cc, j=j):
                        outs[j][:, (1 - cc) * half : (2 - cc) * half] = swap[1, j]
        sems.finish()

    return [p0, a1, every("a2"), every("b1"), every("b2"), end]


def scatter_parts(n, terms):
    side = math.isqrt(n // 2)
    R, W = terms[0].shape
    rows = R // n
    if len(terms) == 1:
        shapes = [(m, W) for _, m in down_split(rows)]
        operands = [terms[0].reshape(side, side, 2, rows, W)]
    else:
        shapes = [(2 * rows, W // 2)] * 2
        operands = [term.reshape(side, side, 2 * rows, W) for term in terms]
    groups = [scatter_scratch(side, r, w) for r, w in shapes]
    count = 2 * 9 + 2
    outs = [jax.ShapeDtypeStruct((rows, W), BF16)] * len(terms)
    scratch = [
        pltpu.VMEM((2, 2, rows, W // 2), BF16),
        pltpu.SemaphoreType.DMA((count,)),
        pltpu.SemaphoreType.DMA((count,)),
        pltpu.SemaphoreType.DMA((2,)),
    ] + [s for group in groups for s in group]
    return operands, outs, [pl.BlockSpec(memory_space=pltpu.VMEM)] * len(terms), scratch, len(groups[0])


class Beside:
    def __init__(self, n, terms, when, cid):
        self.n, self.when, self.on = n, when, terms is not None
        self.operands, self.outs, self.out_specs, self.scratch, self.kind = [], [], [], [], {}
        if self.on:
            self.operands, self.outs, self.out_specs, self.scratch, self.each = scatter_parts(n, terms)
            self.kind = {"collective_id": cid, "has_side_effects": True}

    def start(self, step, steps, terms, outs, scratch):
        if not self.on:
            return lambda: None
        place = Place(self.n)
        pl.when(step == 0)(place.greet)
        swap, send, recv, local, *flat = scratch
        bufs = [flat[i * self.each : (i + 1) * self.each] for i in range(2)]
        phases = scatter_phases(place, send, recv, local, terms, outs, swap, bufs)
        for phase, k in zip(phases, self.when, strict=True):
            if k < steps:
                pl.when(step == k)(phase)

        def rest():
            @pl.when(step == steps - 1)
            def _():
                for phase, k in zip(phases, self.when, strict=True):
                    if k >= steps:
                        phase()

        return rest


def dot(a, b, dims=((1,), (0,))):
    return lax.dot_general(a, b, (dims, ((), ())), preferred_element_type=F32)


ROWS_ROWS, COLS_COLS = ((0,), (0,)), ((1,), (1,))


def sigmoid(t):
    return 0.5 * jnp.tanh(0.5 * t) + 0.5


def scale_of(wide):
    return lax.rsqrt(jnp.mean(wide * wide, -1, keepdims=True) + 1e-6)


def normed(h):
    wide = h.astype(F32)
    return (wide * scale_of(wide)).astype(BF16)


def cut(n, most):
    return max(c for c in range(256, most + 1, 256) if n % c == 0)


HBM = pl.BlockSpec(memory_space=pltpu.HBM)
LIMIT = 62 << 20
TILE = {
    "f_t": 256, "f_c": 2560, "f_when": (5, 7),
    "b_t": 256, "b_c": 2560, "b_when": (0, 2, 4, 7, 8, 8),
    "s_t": 256, "s_c": 2560, "s_when": (0, 3, 6, 8, 8, 8),
    "d_c": 768,
    "g_c": 768, "g_when": (0, 1, 3, 5, 6, 6),
}


def once(shape, index):
    return pl.BlockSpec(shape, index, pipeline_mode=pl.Buffered(1))


def weight_spec(shape, index, pieces):
    return once(shape, index) if pieces == 1 else pl.BlockSpec(shape, index)


def forward(n, h, wg, wu, wd, nexts, cid):
    S, D = h.shape
    F = wg.shape[1]
    T, C = cut(S, TILE["f_t"]), cut(F, TILE["f_c"])
    nt, nc = S // T, F // C
    steps = nt * nc
    when = TILE["f_when"]
    count = 4 * COPIES

    def kernel(h, wg, wu, wd, ig, iu, id_, o, og, ou, od, a, acc, send, recv):
        j = pl.program_id(1)
        step = pl.program_id(0) * nc + j
        place = Place(n)
        pl.when(step == 0)(place.greet)
        flows, _ = gather_flows(place, Sems(send, recv), (og, ou, od), None)

        def every(what):
            def run():
                for flow in flows:
                    getattr(flow, what)()
            return run

        pl.when(step == 0)(every("b1_next"))
        pl.when(step == when[0])(every("b2"))
        pl.when(step == when[1])(every("c1"))

        @pl.when(j == 0)
        def _():
            a[...] = normed(h[...])
            acc[...] = jnp.zeros_like(acc)

        gate, up = dot(a[...], wg[...]), dot(a[...], wu[...])
        act = (gate * sigmoid(gate) * up).astype(BF16)
        acc[...] += dot(act, wd[...])

        @pl.when(j == nc - 1)
        def _():
            o[...] = (h[...].astype(F32) + acc[...].astype(BF16).astype(F32)).astype(BF16)

        @pl.when(step == steps - 1)
        def _():
            every("end")()
            for flow in flows:
                flow.sends(False)

    out = pl.pallas_call(
        kernel,
        grid=(nt, nc),
        out_shape=[jax.ShapeDtypeStruct((S, D), BF16)] + [jax.ShapeDtypeStruct(t.shape, BF16) for t in nexts],
        in_specs=[
            pl.BlockSpec((T, D), lambda i, j: (i, 0)),
            weight_spec((D, C), lambda i, j: (0, j), nc),
            weight_spec((D, C), lambda i, j: (0, j), nc),
            weight_spec((C, D), lambda i, j: (j, 0), nc),
            HBM,
            HBM,
            HBM,
        ],
        out_specs=[pl.BlockSpec((T, D), lambda i, j: (i, 0)), HBM, HBM, HBM],
        scratch_shapes=[
            pltpu.VMEM((T, D), BF16),
            pltpu.VMEM((T, D), F32),
            pltpu.SemaphoreType.DMA((count,)),
            pltpu.SemaphoreType.DMA((count,)),
        ],
        input_output_aliases={4: 1, 5: 2, 6: 3},
        compiler_params=pltpu.CompilerParams(
            collective_id=cid, has_side_effects=True, vmem_limit_bytes=LIMIT, dimension_semantics=("arbitrary", "arbitrary")
        ),
        cost_estimate=pl.CostEstimate(flops=6 * S * D * F, bytes_accessed=4 * S * D, transcendentals=S * F),
        name="forward",
    )(h, wg, wu, wd, *nexts)
    return out[0], out[1:]


def by_normed(h, by_a, dy):
    by_a = by_a.astype(BF16).astype(F32)
    wide = h.astype(F32)
    scale = scale_of(wide)
    hat = wide * scale
    by_wide = scale * (by_a - hat * jnp.mean(by_a * hat, -1, keepdims=True))
    return (dy.astype(F32) + by_wide.astype(BF16).astype(F32)).astype(BF16)


def backward(n, h, dy, wg, wu, wd, full, terms, cid):
    S, D = h.shape
    F = wg.shape[1]
    T, C = cut(S, TILE["b_t"]), cut(F, TILE["b_c"])
    nt, nc = S // T, F // C
    steps = nt * nc
    beside = Beside(n, terms, TILE["b_when"], cid)
    most = 5 if full else 4

    def kernel(h, dy, wg, wu, wd, *rest):
        k = len(beside.operands)
        terms_, rest = rest[:k], rest[k:]
        (act, dg, du, a), dh, rest = rest[:4], rest[most - 1], rest[most:]
        k = len(beside.outs)
        sums, rest = rest[:k], rest[k:]
        acc, rest = (rest[0], rest[1:]) if full else (None, rest)
        j = pl.program_id(1)
        step = pl.program_id(0) * nc + j
        left = beside.start(step, steps, terms_, sums, rest)

        @pl.when(j == 0)
        def _():
            a[...] = normed(h[...])
            if full:
                acc[...] = jnp.zeros_like(acc)

        gate, up = dot(a[...], wg[...]), dot(a[...], wu[...])
        dact = dot(dy[...], wd[...], COLS_COLS).astype(BF16).astype(F32)
        sig = sigmoid(gate)
        silu = gate * sig
        act[...] = (silu * up).astype(BF16)
        by_up = (dact * silu).astype(BF16)
        by_gate = (dact * up * (sig + silu * (1.0 - sig))).astype(BF16)
        du[...] = by_up
        dg[...] = by_gate
        if full:
            acc[...] += dot(by_gate, wg[...], COLS_COLS) + dot(by_up, wu[...], COLS_COLS)

            @pl.when(j == nc - 1)
            def _():
                dh[...] = by_normed(h[...], acc[...], dy[...])

        left()

    tile = pl.BlockSpec((T, D), lambda i, j: (i, 0))
    wide_tile = pl.BlockSpec((T, C), lambda i, j: (i, j))
    out = pl.pallas_call(
        kernel,
        grid=(nt, nc),
        out_shape=[jax.ShapeDtypeStruct((S, F), BF16)] * 3 + [jax.ShapeDtypeStruct((S, D), BF16)] * (most - 3) + beside.outs,
        in_specs=[
            tile,
            tile,
            weight_spec((D, C), lambda i, j: (0, j), nc),
            weight_spec((D, C), lambda i, j: (0, j), nc),
            weight_spec((C, D), lambda i, j: (j, 0), nc),
        ]
        + [HBM] * len(beside.operands),
        out_specs=[wide_tile] * 3 + [tile] * (most - 3) + beside.out_specs,
        scratch_shapes=[pltpu.VMEM((T, D), F32)] * full + beside.scratch,
        compiler_params=pltpu.CompilerParams(vmem_limit_bytes=LIMIT, dimension_semantics=("arbitrary", "arbitrary"), **beside.kind),
        cost_estimate=pl.CostEstimate(flops=10 * S * D * F, bytes_accessed=6 * S * F, transcendentals=S * F),
        name=f"backward{cid}",
    )(h, dy, wg, wu, wd, *beside.operands)
    return out[:most], out[most:]


def to_state(n, h, dy, dg, du, wg, wu, terms, cid):
    S, D = h.shape
    F = wg.shape[1]
    T, C = cut(S, TILE["s_t"]), cut(F, TILE["s_c"])
    nt, nc = S // T, F // C
    steps = nt * nc
    beside = Beside(n, terms, TILE["s_when"], cid)

    def kernel(h, dy, dg, du, wg, wu, *rest):
        k = len(beside.operands)
        terms_, dh, rest = rest[:k], rest[k], rest[k + 1 :]
        k = len(beside.outs)
        sums, acc, rest = rest[:k], rest[k], rest[k + 1 :]
        j = pl.program_id(1)
        step = pl.program_id(0) * nc + j
        left = beside.start(step, steps, terms_, sums, rest)

        @pl.when(j == 0)
        def _():
            acc[...] = jnp.zeros_like(acc)

        acc[...] += dot(dg[...], wg[...], COLS_COLS) + dot(du[...], wu[...], COLS_COLS)

        @pl.when(j == nc - 1)
        def _():
            dh[...] = by_normed(h[...], acc[...], dy[...])

        left()

    tile = pl.BlockSpec((T, D), lambda i, j: (i, 0))
    wide_tile = pl.BlockSpec((T, C), lambda i, j: (i, j))
    weight = weight_spec((D, C), lambda i, j: (0, j), nc)
    out = pl.pallas_call(
        kernel,
        grid=(nt, nc),
        out_shape=[jax.ShapeDtypeStruct((S, D), BF16)] + beside.outs,
        in_specs=[tile, tile, wide_tile, wide_tile, weight, weight] + [HBM] * len(beside.operands),
        out_specs=[tile] + beside.out_specs,
        scratch_shapes=[pltpu.VMEM((T, D), F32)] + beside.scratch,
        compiler_params=pltpu.CompilerParams(vmem_limit_bytes=LIMIT, dimension_semantics=("arbitrary", "arbitrary"), **beside.kind),
        cost_estimate=pl.CostEstimate(flops=4 * S * D * F, bytes_accessed=4 * S * F, transcendentals=0),
        name="to_state",
    )(h, dy, dg, du, wg, wu, *beside.operands)
    return out[0], out[1:]


def down_weight(act, dy):
    S, D = dy.shape
    F = act.shape[1]
    C = cut(F, TILE["d_c"])

    def kernel(act, dy, od):
        od[...] = dot(act[...], dy[...], ROWS_ROWS).astype(BF16)

    return pl.pallas_call(
        kernel,
        grid=(F // C,),
        out_shape=jax.ShapeDtypeStruct((F, D), BF16),
        in_specs=[pl.BlockSpec((S, C), lambda i: (0, i)), once((S, D), lambda i: (0, 0))],
        out_specs=pl.BlockSpec((C, D), lambda i: (i, 0)),
        compiler_params=pltpu.CompilerParams(vmem_limit_bytes=LIMIT, dimension_semantics=("arbitrary",)),
        cost_estimate=pl.CostEstimate(flops=2 * S * D * F, bytes_accessed=2 * S * F, transcendentals=0),
        name="down_weight",
    )(act, dy)


def gate_weights(n, a, dg, du, terms, cid):
    S, D = a.shape
    F = dg.shape[1]
    C = cut(F, TILE["g_c"])
    nc = F // C
    steps = 2 * nc
    beside = Beside(n, terms, TILE["g_when"], cid)

    def kernel(a, dg, du, *rest):
        k = len(beside.operands)
        terms_, og, ou, rest = rest[:k], rest[k], rest[k + 1], rest[k + 2 :]
        k = len(beside.outs)
        sums, rest = rest[:k], rest[k:]
        step = pl.program_id(0)
        left = beside.start(step, steps, terms_, sums, rest)

        @pl.when(step < nc)
        def _():
            og[...] = dot(a[...], dg[...], ROWS_ROWS).astype(BF16)

        @pl.when(step >= nc)
        def _():
            ou[...] = dot(a[...], du[...], ROWS_ROWS).astype(BF16)

        left()

    def cols(k, rows):
        return pl.BlockSpec((rows, C), lambda i: (0, jnp.clip(i - k * nc, 0, nc - 1)))

    out = pl.pallas_call(
        kernel,
        grid=(steps,),
        out_shape=[jax.ShapeDtypeStruct((D, F), BF16)] * 2 + beside.outs,
        in_specs=[once((S, D), lambda i: (0, 0)), cols(0, S), cols(1, S)] + [HBM] * len(beside.operands),
        out_specs=[cols(0, D), cols(1, D)] + beside.out_specs,
        scratch_shapes=beside.scratch,
        compiler_params=pltpu.CompilerParams(vmem_limit_bytes=LIMIT, dimension_semantics=("arbitrary",), **beside.kind),
        cost_estimate=pl.CostEstimate(flops=4 * S * D * F, bytes_accessed=4 * S * F, transcendentals=0),
        name=f"gate_weights{cid}",
    )(a, dg, du, *beside.operands)
    return out[:2], out[2:]


def solution(mesh):
    n = mesh.shape["dp"]

    def device(x, dy, wg, wu, wd):
        x, dy = x.reshape(x.shape[1:]), dy.reshape(dy.shape[1:])
        first, nexts = gather(n, wg, wu, wd, 0)
        w0 = whole(n, first)
        h, second = forward(n, x, *w0, nexts, 1)
        w1 = whole(n, second)

        (act, dg, du, a, dh), _ = backward(n, h, dy, *w1, True, None, 2)
        down = down_weight(act, dy)
        gates, (down1,) = gate_weights(n, a, dg, du, [down], 3)

        (act, dg, du, a), gates1 = backward(n, x, dh, *w0, False, gates, 4)
        down = down_weight(act, dh)
        gates, (down0,) = gate_weights(n, a, dg, du, [down], 5)
        dx, gates0 = to_state(n, x, dh, dg, du, *w0[:2], gates, 6)
        sums = [(*gates0, down0), (*gates1, down1)]
        return (dx[None], *(jnp.stack([s[j] for s in sums]) for j in range(3)))

    tokens, rows = P(("rep", "dp")), P(None, "dp")
    return jax.shard_map(
        device, mesh=mesh, in_specs=(tokens, tokens, rows, rows, rows), out_specs=(tokens, *[P("rep", "dp")] * 3), check_vma=False
    )
```

time: 379 us -> 374 us (0.987)
  Pallas kernels: 367 us -> 358 us
    pallas_call x2, Pallas kernels: 146 us -> 113 us  [backward(): pl.pallas_call(kernel, grid=(nt, nc), out_shape=[jax.ShapeDtypeStruct((S,...]
    pallas_call x4 -> x6, Pallas kernels: 169 us -> 201 us  [the longest x2 68.4 us: gate_weights(): pl.pallas_call(kernel, grid=(steps,), out_shape=[jax.ShapeDtypeStruct((D,...]
    pallas_call x1, Pallas kernels: 52.3 us -> 43.3 us  [forward(): pl.pallas_call(kernel, grid=(nt, nc), out_shape=[jax.ShapeDtypeStruct((S,...]
where the time goes in v3:
time: 374 us; the launch traced here: 371 us
  Pallas kernels  358 us (96%)
  local copies, waits for them, and re-layouts  9.49 us (3%)
    pallas_call x2, Pallas kernels, backward(): pl.pallas_call(kernel, grid=(nt, nc), out_shape=[jax.ShapeDtypeStruct((S,...  113 us
    pallas_call x2, Pallas kernels, gate_weights(): pl.pallas_call(kernel, grid=(steps,), out_shape=[jax.ShapeDtypeStruct((D,...  68.4 us
    pallas_call x1, Pallas kernels, gather(): pl.pallas_call(kernel, out_shape=gather_shapes(n, rows, F, drows, D) * la...  52.7 us
    pallas_call x1, Pallas kernels, to_state(): pl.pallas_call(kernel, grid=(nt, nc), out_shape=[jax.ShapeDtypeStruct((S,...  51.1 us
    pallas_call x1, Pallas kernels, forward(): pl.pallas_call(kernel, grid=(nt, nc), out_shape=[jax.ShapeDtypeStruct((S,...  43.3 us
    pallas_call x2, Pallas kernels, down_weight(): pl.pallas_call(kernel, grid=(F // C,), out_shape=jax.ShapeDtypeStruct((F,...  29.2 us
    unnamed x13, local copies, waits for them, and re-layouts  9.49 us

profile of v3, /device:TPU:97, one launch (start us, length us, event | category | flops | bytes accessed | tf_op | source)
XLA Modules:
  0.0 370.9 jit_solution(5793021850871110950)
XLA Ops:
  0.6 1.7 copy.12.wg
  2.3 1.7 copy.13.wu
  4.0 52.7 %gather.1 = (bf16[4,4,56,2304]{3,2,1,0:T(8,128)(2,1)}, bf16[4,4,56,2304]{3,2,1,0:T(8,128)(2,1)}, bf16[4,4,2,72,896]{4,3,2,1,0:T(8,128)(2,1)}, bf16[4,4,56,2304]{...) custom-call(bf16[2,28,2304]{2,1,0:T(8,128)(2,1)} %copy.12.wg, ...), custom_call_target="tpu_custom_call" | custom-call | tf_op jit(solution)/shard_map/gather/pallas_call | solution.py:241
  56.7 43.3 %forward.1 = (bf16[2048,896]{1,0:T(8,128)(2,1)}, bf16[4,4,56,2304]{3,2,1,0:T(8,128)(2,1)}, bf16[4,4,56,2304]{3,2,1,0:T(8,128)(2,1)}, bf16[4,4,2,72,896]{4,3,2,1,0:T(8,128)(2,1)}) custom-call(bf16[2048,896]{1,0:T(8,128)(2,1)} %bitcast.41, bf16[896,2304]{1,0:T(8,128)(2,1)} %bitcast.28, ...), custom_call_target="tpu_custom_call", output_to_operand_aliasing={{1}: (4, {}), {2}: (5, {}), {3}: (6, {})} | custom-call | flops 25367150592 | bytes 7340032 | tf_op jit(solution)/shard_map/forward/pallas_call | solution.py:560
  100.0 61.4 %backward2.1 = (bf16[2048,2304]{1,0:T(8,128)(2,1)}, bf16[2048,2304]{1,0:T(8,128)(2,1)}, bf16[2048,2304]{1,0:T(8,128)(2,1)}, bf16[2048,896]{1,0:T(8,128)(2,1)}, bf16[2048,896]{1,0:T(8,128)(2,1)}) custom-call(bf16[2048,896]{1,0:T(8,128)(2,1)} %get-tuple-element.40.h, bf16[2048,896]{1,0:T(8,128)(2,1)} %bitcast.39, bf16[896,2304]{1,0:T(8,128)(2,1)} %bitcast.36, ...), custom_call_target="tpu_custom_call" | custom-call | flops 42278584320 | bytes 28311552 | tf_op jit(solution)/shard_map/backward2/pallas_call | solution.py:645
  161.4 14.4 %down_weight.2 = bf16[2304,896]{1,0:T(8,128)(2,1)} custom-call(bf16[2048,2304]{1,0:T(8,128)(2,1)} %get-tuple-element.48.act, bf16[2048,896]{1,0:T(8,128)(2,1)} %bitcast.40), custom_call_target="tpu_custom_call" | custom-call | flops 8455716864 | bytes 9437184 | tf_op jit(solution)/shard_map/down_weight/pallas_call | solution.py:720
  175.8 35.3 %gate_weights3.1 = (bf16[896,2304]{1,0:T(8,128)(2,1)}, bf16[896,2304]{1,0:T(8,128)(2,1)}, bf16[72,896]{1,0:T(8,128)(2,1)}) custom-call(bf16[2048,896]{1,0:T(8,128)(2,1)} %get-tuple-element.45.a, bf16[2048,2304]{1,0:T(8,128)(2,1)} %get-tuple-element.46.dg, bf16[2048,2304]{1,0:T(8,128)(2,1)} %get-tuple-element.47.du, bf16[4,4,2,72,896]{4,3,2,1,0:T(8,128)(2,1)} %bitcast.48), custom_call_target="tpu_custom_call" | custom-call | flops 16911433728 | bytes 18874368 | tf_op jit(solution)/shard_map/gate_weights3/pallas_call | solution.py:761
  211.1 51.7 %backward4.1 = (bf16[2048,2304]{1,0:T(8,128)(2,1)}, bf16[2048,2304]{1,0:T(8,128)(2,1)}, bf16[2048,2304]{1,0:T(8,128)(2,1)}, bf16[2048,896]{1,0:T(8,128)(2,1)}, b...) custom-call(bf16[2048,896]{1,0:T(8,128)(2,1)} %bitcast.42, bf16[2048,896]{1,0:T(8,128)(2,1)} %get-tuple-element.44.dy, ...), custom_call_target="tpu_custom_call" | custom-call | flops 42278584320 | bytes 28311552 | tf_op jit(solution)/shard_map/backward4/pallas_call | solution.py:645
  262.8 14.7 %down_weight.3 = bf16[2304,896]{1,0:T(8,128)(2,1)} custom-call(bf16[2048,2304]{1,0:T(8,128)(2,1)} %get-tuple-element.54.act, bf16[2048,896]{1,0:T(8,128)(2,1)} %get-tuple-element.44.dy), custom_call_target="tpu_custom_call" | custom-call | flops 8455716864 | bytes 9437184 | tf_op jit(solution)/shard_map/down_weight/pallas_call | solution.py:720
  277.5 33.1 %gate_weights5.1 = (bf16[896,2304]{1,0:T(8,128)(2,1)}, bf16[896,2304]{1,0:T(8,128)(2,1)}, bf16[72,896]{1,0:T(8,128)(2,1)}) custom-call(bf16[2048,896]{1,0:T(8,128)(2,1)} %get-tuple-element.53.a, bf16[2048,2304]{1,0:T(8,128)(2,1)} %get-tuple-element.51.dg, bf16[2048,2304]{1,0:T(8,128)(2,1)} %get-tuple-element.52.du, bf16[4,4,2,72,896]{4,3,2,1,0:T(8,128)(2,1)} %bitcast.49), custom_call_target="tpu_custom_call" | custom-call | flops 16911433728 | bytes 18874368 | tf_op jit(solution)/shard_map/gate_weights5/pallas_call | solution.py:761
  310.6 0.0 copy-start.1
  310.6 0.0 copy-start.2
  310.6 0.0 copy-start.3
  310.6 0.0 copy-start
  310.6 51.1 %to_state.1 = (bf16[2048,896]{1,0:T(8,128)(2,1)}, bf16[28,2304]{1,0:T(8,128)(2,1)}, bf16[28,2304]{1,0:T(8,128)(2,1)}) custom-call(bf16[2048,896]{1,0:T(8,128)(2,1)} %bitcast.43, bf16[2048,896]{1,0:T(8,128)(2,1)} %get-tuple-element.44.dy, bf16[2048,2304]{1,0:T(8,128)(2,1)} %get-tuple-element.51.dg, bf16[2048,2304]{1,0:T(8,128)(2,1)} %get-tuple-element.52.du, ...), custom_call_target="tpu_custom_call" | custom-call | flops 16911433728 | bytes 18874368 | tf_op jit(solution)/shard_map/to_state/pallas_call | solution.py:698
  361.7 0.0 copy-done.1
  361.7 0.9 pad_maximum_fusion
  362.7 1.0 copy.14
  363.6 0.0 copy-done.2
  363.6 0.0 copy-done.3
  363.6 0.7 pad_maximum_fusion.2
  364.4 0.9 pad_maximum_fusion.1
  365.3 1.0 copy.15
  366.3 4.2 %copy.20 = bf16[1,2048,896]{2,1,0:T(8,128)(2,1)} copy(bf16[1,2048,896]{2,1,0:T(8,128)(2,1)} %bitcast.21) | data formatting | bytes 7340032
  (1 shorter events, 0.0 us)
Async XLA Ops:
  310.6 51.1 %copy-start.1 = (bf16[28,2304]{1,0:T(8,128)(2,1)S(1)}, bf16[28,2304]{1,0:T(8,128)(2,1)}, u32[]{:S(2)}) copy-start(bf16[28,2304]{1,0:T(8,128)(2,1)} %get-tuple-element.59) | copy-start | bytes 387076
  310.6 53.0 %copy-start.2 = (bf16[72,896]{1,0:T(8,128)(2,1)S(1)}, bf16[72,896]{1,0:T(8,128)(2,1)}, u32[]{:S(2)}) copy-start(bf16[72,896]{1,0:T(8,128)(2,1)} %get-tuple-element.63) | copy-start | bytes 387076
  310.6 53.0 %copy-start.3 = (bf16[72,896]{1,0:T(8,128)(2,1)S(1)}, bf16[72,896]{1,0:T(8,128)(2,1)}, u32[]{:S(2)}) copy-start(bf16[72,896]{1,0:T(8,128)(2,1)} %get-tuple-element.62) | copy-start | bytes 387076
  310.6 53.7 %copy-start = (bf16[28,2304]{1,0:T(8,128)(2,1)S(1)}, bf16[28,2304]{1,0:T(8,128)(2,1)}, u32[]{:S(2)}) copy-start(bf16[28,2304]{1,0:T(8,128)(2,1)} %get-tuple-element.61) | copy-start | bytes 387076

commit v4 on v3

--- a/solution.py
+++ b/solution.py
@@ -361,14 +361,15 @@
 def scatter_phases(place, send, recv, local, terms, outs, swap, bufs):
     c = place.c
     sems = Sems(send, recv)
-    down = len(terms) == 1
-    half = terms[0].shape[-1] // 2
+    terms = terms[0]
+    down = len(outs) == 1
+    half = terms.shape[-1] // 2
 
     def share(who):
         if down:
-            return [terms[0].at[:, :, who, pl.ds(lo, m), :] for lo, m in down_split(terms[0].shape[3])]
+            return [terms.at[:, :, who, pl.ds(lo, m), :] for lo, m in down_split(terms.shape[3])]
         lanes = pl.ds(pl.multiple_of(who * half, 128), half)
-        return [term.at[:, :, :, lanes] for term in terms]
+        return [terms.at[j, :, :, :, lanes] for j in (0, 1)]
 
     flows = [Scatter(place, sems, axis, *buf) for axis, buf in enumerate(bufs)]
     first = [sems.copy(theirs, flow.l1, place.partner) for theirs, flow in zip(share(1 - c), flows, strict=True)]
@@ -393,7 +394,7 @@
 
     def end():
         if down:
-            for (lo, m), flow in zip(down_split(terms[0].shape[3]), flows, strict=True):
+            for (lo, m), flow in zip(down_split(terms.shape[3]), flows, strict=True):
                 outs[0][pl.ds(lo, m), :] = flow.last().astype(BF16)
         else:
             rows = outs[0].shape[0]
@@ -419,24 +420,24 @@
 
 def scatter_parts(n, terms):
     side = math.isqrt(n // 2)
-    R, W = terms[0].shape
+    R, W = terms.shape[-2:]
     rows = R // n
-    if len(terms) == 1:
+    if terms.ndim == 2:
         shapes = [(m, W) for _, m in down_split(rows)]
-        operands = [terms[0].reshape(side, side, 2, rows, W)]
+        operands = [terms.reshape(side, side, 2, rows, W)]
     else:
         shapes = [(2 * rows, W // 2)] * 2
-        operands = [term.reshape(side, side, 2 * rows, W) for term in terms]
+        operands = [terms.reshape(2, side, side, 2 * rows, W)]
     groups = [scatter_scratch(side, r, w) for r, w in shapes]
     count = 2 * 9 + 2
-    outs = [jax.ShapeDtypeStruct((rows, W), BF16)] * len(terms)
+    outs = [jax.ShapeDtypeStruct((rows, W), BF16)] * (terms.ndim - 1)
     scratch = [
         pltpu.VMEM((2, 2, rows, W // 2), BF16),
         pltpu.SemaphoreType.DMA((count,)),
         pltpu.SemaphoreType.DMA((count,)),
         pltpu.SemaphoreType.DMA((2,)),
     ] + [s for group in groups for s in group]
-    return operands, outs, [pl.BlockSpec(memory_space=pltpu.VMEM)] * len(terms), scratch, len(groups[0])
+    return operands, outs, [pl.BlockSpec(memory_space=pltpu.VMEM)] * len(outs), scratch, len(groups[0])
 
 
 class Beside:
@@ -496,11 +497,11 @@
 HBM = pl.BlockSpec(memory_space=pltpu.HBM)
 LIMIT = 62 << 20
 TILE = {
-    "f_t": 256, "f_c": 2560, "f_when": (5, 7),
-    "b_t": 256, "b_c": 2560, "b_when": (0, 2, 4, 7, 8, 8),
-    "s_t": 256, "s_c": 2560, "s_when": (0, 3, 6, 8, 8, 8),
+    "f_t": 256, "f_c": 2560, "f_when": (4, 7),
+    "b_t": 256, "b_c": 2560, "b_when": (0, 1, 3, 6, 7, 8),
+    "s_t": 256, "s_c": 2560, "s_when": (0, 2, 4, 8, 8, 8),
     "d_c": 768,
-    "g_c": 768, "g_when": (0, 1, 3, 5, 6, 6),
+    "g_c": 768, "g_when": (0, 1, 2, 4, 5, 6),
 }
 
 
@@ -603,12 +604,12 @@
     nt, nc = S // T, F // C
     steps = nt * nc
     beside = Beside(n, terms, TILE["b_when"], cid)
-    most = 5 if full else 4
+    most = 4 if full else 3
 
     def kernel(h, dy, wg, wu, wd, *rest):
         k = len(beside.operands)
         terms_, rest = rest[:k], rest[k:]
-        (act, dg, du, a), dh, rest = rest[:4], rest[most - 1], rest[most:]
+        (act, dgu, a), dh, rest = rest[:3], rest[most - 1], rest[most:]
         k = len(beside.outs)
         sums, rest = rest[:k], rest[k:]
         acc, rest = (rest[0], rest[1:]) if full else (None, rest)
@@ -629,8 +630,8 @@
         act[...] = (silu * up).astype(BF16)
         by_up = (dact * silu).astype(BF16)
         by_gate = (dact * up * (sig + silu * (1.0 - sig))).astype(BF16)
-        du[...] = by_up
-        dg[...] = by_gate
+        dgu[0] = by_gate
+        dgu[1] = by_up
         if full:
             acc[...] += dot(by_gate, wg[...], COLS_COLS) + dot(by_up, wu[...], COLS_COLS)
 
@@ -645,7 +646,9 @@
     out = pl.pallas_call(
         kernel,
         grid=(nt, nc),
-        out_shape=[jax.ShapeDtypeStruct((S, F), BF16)] * 3 + [jax.ShapeDtypeStruct((S, D), BF16)] * (most - 3) + beside.outs,
+        out_shape=[jax.ShapeDtypeStruct((S, F), BF16), jax.ShapeDtypeStruct((2, S, F), BF16)]
+        + [jax.ShapeDtypeStruct((S, D), BF16)] * (most - 2)
+        + beside.outs,
         in_specs=[
             tile,
             tile,
@@ -654,7 +657,7 @@
             weight_spec((C, D), lambda i, j: (j, 0), nc),
         ]
         + [HBM] * len(beside.operands),
-        out_specs=[wide_tile] * 3 + [tile] * (most - 3) + beside.out_specs,
+        out_specs=[wide_tile, pl.BlockSpec((2, T, C), lambda i, j: (0, i, j))] + [tile] * (most - 2) + beside.out_specs,
         scratch_shapes=[pltpu.VMEM((T, D), F32)] * full + beside.scratch,
         compiler_params=pltpu.CompilerParams(vmem_limit_bytes=LIMIT, dimension_semantics=("arbitrary", "arbitrary"), **beside.kind),
         cost_estimate=pl.CostEstimate(flops=10 * S * D * F, bytes_accessed=6 * S * F, transcendentals=S * F),
@@ -663,7 +666,7 @@
     return out[:most], out[most:]
 
 
-def to_state(n, h, dy, dg, du, wg, wu, terms, cid):
+def to_state(n, h, dy, dgu, wg, wu, terms, cid):
     S, D = h.shape
     F = wg.shape[1]
     T, C = cut(S, TILE["s_t"]), cut(F, TILE["s_c"])
@@ -671,7 +674,7 @@
     steps = nt * nc
     beside = Beside(n, terms, TILE["s_when"], cid)
 
-    def kernel(h, dy, dg, du, wg, wu, *rest):
+    def kernel(h, dy, dgu, wg, wu, *rest):
         k = len(beside.operands)
         terms_, dh, rest = rest[:k], rest[k], rest[k + 1 :]
         k = len(beside.outs)
@@ -684,7 +687,7 @@
         def _():
             acc[...] = jnp.zeros_like(acc)
 
-        acc[...] += dot(dg[...], wg[...], COLS_COLS) + dot(du[...], wu[...], COLS_COLS)
+        acc[...] += dot(dgu[0], wg[...], COLS_COLS) + dot(dgu[1], wu[...], COLS_COLS)
 
         @pl.when(j == nc - 1)
         def _():
@@ -693,19 +696,19 @@
         left()
 
     tile = pl.BlockSpec((T, D), lambda i, j: (i, 0))
-    wide_tile = pl.BlockSpec((T, C), lambda i, j: (i, j))
+    wide_tile = pl.BlockSpec((2, T, C), lambda i, j: (0, i, j))
     weight = weight_spec((D, C), lambda i, j: (0, j), nc)
     out = pl.pallas_call(
         kernel,
         grid=(nt, nc),
         out_shape=[jax.ShapeDtypeStruct((S, D), BF16)] + beside.outs,
-        in_specs=[tile, tile, wide_tile, wide_tile, weight, weight] + [HBM] * len(beside.operands),
+        in_specs=[tile, tile, wide_tile, weight, weight] + [HBM] * len(beside.operands),
         out_specs=[tile] + beside.out_specs,
         scratch_shapes=[pltpu.VMEM((T, D), F32)] + beside.scratch,
         compiler_params=pltpu.CompilerParams(vmem_limit_bytes=LIMIT, dimension_semantics=("arbitrary", "arbitrary"), **beside.kind),
         cost_estimate=pl.CostEstimate(flops=4 * S * D * F, bytes_accessed=4 * S * F, transcendentals=0),
         name="to_state",
-    )(h, dy, dg, du, wg, wu, *beside.operands)
+    )(h, dy, dgu, wg, wu, *beside.operands)
     return out[0], out[1:]
 
 
@@ -729,47 +732,36 @@
     )(act, dy)
 
 
-def gate_weights(n, a, dg, du, terms, cid):
+def gate_weights(n, a, dgu, terms, cid):
     S, D = a.shape
-    F = dg.shape[1]
+    F = dgu.shape[2]
     C = cut(F, TILE["g_c"])
     nc = F // C
     steps = 2 * nc
     beside = Beside(n, terms, TILE["g_when"], cid)
 
-    def kernel(a, dg, du, *rest):
+    def kernel(a, dgu, *rest):
         k = len(beside.operands)
-        terms_, og, ou, rest = rest[:k], rest[k], rest[k + 1], rest[k + 2 :]
+        terms_, o, rest = rest[:k], rest[k], rest[k + 1 :]
         k = len(beside.outs)
         sums, rest = rest[:k], rest[k:]
-        step = pl.program_id(0)
+        step = pl.program_id(0) * nc + pl.program_id(1)
         left = beside.start(step, steps, terms_, sums, rest)
-
-        @pl.when(step < nc)
-        def _():
-            og[...] = dot(a[...], dg[...], ROWS_ROWS).astype(BF16)
-
-        @pl.when(step >= nc)
-        def _():
-            ou[...] = dot(a[...], du[...], ROWS_ROWS).astype(BF16)
-
+        o[...] = dot(a[...], dgu[...], ROWS_ROWS).astype(BF16)
         left()
-
-    def cols(k, rows):
-        return pl.BlockSpec((rows, C), lambda i: (0, jnp.clip(i - k * nc, 0, nc - 1)))
 
     out = pl.pallas_call(
         kernel,
-        grid=(steps,),
-        out_shape=[jax.ShapeDtypeStruct((D, F), BF16)] * 2 + beside.outs,
-        in_specs=[once((S, D), lambda i: (0, 0)), cols(0, S), cols(1, S)] + [HBM] * len(beside.operands),
-        out_specs=[cols(0, D), cols(1, D)] + beside.out_specs,
+        grid=(2, nc),
+        out_shape=[jax.ShapeDtypeStruct((2, D, F), BF16)] + beside.outs,
+        in_specs=[once((S, D), lambda k, j: (0, 0)), pl.BlockSpec((None, S, C), lambda k, j: (k, 0, j))] + [HBM] * len(beside.operands),
+        out_specs=[pl.BlockSpec((None, D, C), lambda k, j: (k, 0, j))] + beside.out_specs,
         scratch_shapes=beside.scratch,
-        compiler_params=pltpu.CompilerParams(vmem_limit_bytes=LIMIT, dimension_semantics=("arbitrary",), **beside.kind),
+        compiler_params=pltpu.CompilerParams(vmem_limit_bytes=LIMIT, dimension_semantics=("arbitrary", "arbitrary"), **beside.kind),
         cost_estimate=pl.CostEstimate(flops=4 * S * D * F, bytes_accessed=4 * S * F, transcendentals=0),
         name=f"gate_weights{cid}",
-    )(a, dg, du, *beside.operands)
-    return out[:2], out[2:]
+    )(a, dgu, *beside.operands)
+    return out[0], out[1:]
 
 
 def solution(mesh):
@@ -782,14 +774,14 @@
         h, second = forward(n, x, *w0, nexts, 1)
         w1 = whole(n, second)
 
-        (act, dg, du, a, dh), _ = backward(n, h, dy, *w1, True, None, 2)
+        (act, dgu, a, dh), _ = backward(n, h, dy, *w1, True, None, 2)
         down = down_weight(act, dy)
-        gates, (down1,) = gate_weights(n, a, dg, du, [down], 3)
-
-        (act, dg, du, a), gates1 = backward(n, x, dh, *w0, False, gates, 4)
+        gates, (down1,) = gate_weights(n, a, dgu, down, 3)
+
+        (act, dgu, a), gates1 = backward(n, x, dh, *w0, False, gates, 4)
         down = down_weight(act, dh)
-        gates, (down0,) = gate_weights(n, a, dg, du, [down], 5)
-        dx, gates0 = to_state(n, x, dh, dg, du, *w0[:2], gates, 6)
+        gates, (down0,) = gate_weights(n, a, dgu, down, 5)
+        dx, gates0 = to_state(n, x, dh, dgu, *w0[:2], gates, 6)
         sums = [(*gates0, down0), (*gates1, down1)]
         return (dx[None], *(jnp.stack([s[j] for s in sums]) for j in range(3)))
 

time: 374 us -> 358 us (0.957)
  Pallas kernels: 358 us -> 345 us
    pallas_call x2, Pallas kernels: 68.4 us -> 60 us  [gate_weights(): pl.pallas_call(kernel, grid=(2, nc), out_shape=[jax.ShapeDtypeStruct((2,...]
    pallas_call x1, Pallas kernels: 51.1 us -> 47.1 us  [to_state(): pl.pallas_call(kernel, grid=(nt, nc), out_shape=[jax.ShapeDtypeStruct((S,...]
where the time goes in v4:
time: 358 us; the launch traced here: 357 us
  Pallas kernels  345 us (96%)
  local copies, waits for them, and re-layouts  9.49 us (3%)
    pallas_call x2, Pallas kernels, backward(): pl.pallas_call(kernel, grid=(nt, nc), out_shape=[jax.ShapeDtypeStruct((S,...  112 us
    pallas_call x2, Pallas kernels, gate_weights(): pl.pallas_call(kernel, grid=(2, nc), out_shape=[jax.ShapeDtypeStruct((2,...  60 us
    pallas_call x1, Pallas kernels, gather(): pl.pallas_call(kernel, out_shape=gather_shapes(n, rows, F, drows, D) * la...  52.7 us
    pallas_call x1, Pallas kernels, to_state(): pl.pallas_call(kernel, grid=(nt, nc), out_shape=[jax.ShapeDtypeStruct((S,...  47.1 us
    pallas_call x1, Pallas kernels, forward(): pl.pallas_call(kernel, grid=(nt, nc), out_shape=[jax.ShapeDtypeStruct((S,...  43.9 us
    pallas_call x2, Pallas kernels, down_weight(): pl.pallas_call(kernel, grid=(F // C,), out_shape=jax.ShapeDtypeStruct((F,...  28.9 us
    unnamed x13, local copies, waits for them, and re-layouts  9.49 us

profile of v4, /device:TPU:97, one launch (start us, length us, event | category | flops | bytes accessed | tf_op | source)
XLA Modules:
  0.0 357.4 jit_solution(13764584191589368316)
XLA Ops:
  0.6 1.7 copy.12.wg
  2.3 1.7 copy.13.wu
  4.0 52.7 %gather.1 = (bf16[4,4,56,2304]{3,2,1,0:T(8,128)(2,1)}, bf16[4,4,56,2304]{3,2,1,0:T(8,128)(2,1)}, bf16[4,4,2,72,896]{4,3,2,1,0:T(8,128)(2,1)}, bf16[4,4,56,2304]{...) custom-call(bf16[2,28,2304]{2,1,0:T(8,128)(2,1)} %copy.12.wg, ...), custom_call_target="tpu_custom_call" | custom-call | tf_op jit(solution)/shard_map/gather/pallas_call | solution.py:241
  56.7 43.9 %forward.1 = (bf16[2048,896]{1,0:T(8,128)(2,1)}, bf16[4,4,56,2304]{3,2,1,0:T(8,128)(2,1)}, bf16[4,4,56,2304]{3,2,1,0:T(8,128)(2,1)}, bf16[4,4,2,72,896]{4,3,2,1,0:T(8,128)(2,1)}) custom-call(bf16[2048,896]{1,0:T(8,128)(2,1)} %bitcast.39, bf16[896,2304]{1,0:T(8,128)(2,1)} %bitcast.26, ...), custom_call_target="tpu_custom_call", output_to_operand_aliasing={{1}: (4, {}), {2}: (5, {}), {3}: (6, {})} | custom-call | flops 25367150592 | bytes 7340032 | tf_op jit(solution)/shard_map/forward/pallas_call | solution.py:561
  100.7 62.3 %backward2.1 = (bf16[2048,2304]{1,0:T(8,128)(2,1)}, bf16[2,2048,2304]{2,1,0:T(8,128)(2,1)}, bf16[2048,896]{1,0:T(8,128)(2,1)}, bf16[2048,896]{1,0:T(8,128)(2,1)}) custom-call(bf16[2048,896]{1,0:T(8,128)(2,1)} %get-tuple-element.36.h, bf16[2048,896]{1,0:T(8,128)(2,1)} %bitcast.37, bf16[896,2304]{1,0:T(8,128)(2,1)} %bitcast.34, bf16[896,2304]{1,0:T(8,128)(2,1)} %bitcast.35, ...), custom_call_target="tpu_custom_call" | custom-call | flops 42278584320 | bytes 28311552 | tf_op jit(solution)/shard_map/backward2/pallas_call | solution.py:646
  163.0 14.4 %down_weight.2 = bf16[2304,896]{1,0:T(8,128)(2,1)} custom-call(bf16[2048,2304]{1,0:T(8,128)(2,1)} %get-tuple-element.43.act, bf16[2048,896]{1,0:T(8,128)(2,1)} %bitcast.38), custom_call_target="tpu_custom_call" | custom-call | flops 8455716864 | bytes 9437184 | tf_op jit(solution)/shard_map/down_weight/pallas_call | solution.py:723
  177.4 31.0 %gate_weights3.1 = (bf16[2,896,2304]{2,1,0:T(8,128)(2,1)}, bf16[72,896]{1,0:T(8,128)(2,1)}) custom-call(bf16[2048,896]{1,0:T(8,128)(2,1)} %get-tuple-element.41.a, bf16[2,2048,2304]{2,1,0:T(8,128)(2,1)} %get-tuple-element.42.dgu, bf16[4,4,2,72,896]{4,3,2,1,0:T(8,128)(2,1)} %bitcast.44), custom_call_target="tpu_custom_call" | custom-call | flops 16911433728 | bytes 18874368 | tf_op jit(solution)/shard_map/gate_weights3/pallas_call | solution.py:753
  208.5 49.5 %backward4.1 = (bf16[2048,2304]{1,0:T(8,128)(2,1)}, bf16[2,2048,2304]{2,1,0:T(8,128)(2,1)}, bf16[2048,896]{1,0:T(8,128)(2,1)}, bf16[28,2304]{1,0:T(8,128)(2,1)}, bf16[28,2304]{1,0:T(8,128)(2,1)}) custom-call(bf16[2048,896]{1,0:T(8,128)(2,1)} %bitcast.40, bf16[2048,896]{1,0:T(8,128)(2,1)} %get-tuple-element.40.dy, bf16[896,2304]{1,0:T(8,128)(2,1)} %bitcast.27, ...), custom_call_target="tpu_custom_call" | custom-call | flops 42278584320 | bytes 28311552 | tf_op jit(solution)/shard_map/backward4/pallas_call | solution.py:646
  258.0 14.5 %down_weight.3 = bf16[2304,896]{1,0:T(8,128)(2,1)} custom-call(bf16[2048,2304]{1,0:T(8,128)(2,1)} %get-tuple-element.47.act, bf16[2048,896]{1,0:T(8,128)(2,1)} %get-tuple-element.40.dy), custom_call_target="tpu_custom_call" | custom-call | flops 8455716864 | bytes 9437184 | tf_op jit(solution)/shard_map/down_weight/pallas_call | solution.py:723
  272.5 29.0 %gate_weights5.1 = (bf16[2,896,2304]{2,1,0:T(8,128)(2,1)}, bf16[72,896]{1,0:T(8,128)(2,1)}) custom-call(bf16[2048,896]{1,0:T(8,128)(2,1)} %get-tuple-element.46.a, bf16[2,2048,2304]{2,1,0:T(8,128)(2,1)} %get-tuple-element.45.dgu, bf16[4,4,2,72,896]{4,3,2,1,0:T(8,128)(2,1)} %bitcast.45), custom_call_target="tpu_custom_call" | custom-call | flops 16911433728 | bytes 18874368 | tf_op jit(solution)/shard_map/gate_weights5/pallas_call | solution.py:753
  301.5 0.0 copy-start.1
  301.5 0.0 copy-start.2
  301.5 0.0 copy-start.3
  301.5 0.0 copy-start
  301.5 47.1 %to_state.1 = (bf16[2048,896]{1,0:T(8,128)(2,1)}, bf16[28,2304]{1,0:T(8,128)(2,1)}, bf16[28,2304]{1,0:T(8,128)(2,1)}) custom-call(bf16[2048,896]{1,0:T(8,128)(2,1)} %bitcast.41, bf16[2048,896]{1,0:T(8,128)(2,1)} %get-tuple-element.40.dy, bf16[2,2048,2304]{2,1,0:T(8,128)(2,1)} %get-tuple-element.45.dgu, bf16[896,2304]{1,0:T(8,128)(2,1)} %bitcast.28, ...), custom_call_target="tpu_custom_call" | custom-call | flops 16911433728 | bytes 18874368 | tf_op jit(solution)/shard_map/to_state/pallas_call | solution.py:701
  348.7 0.0 copy-done.1
  348.7 0.9 pad_maximum_fusion
  349.6 1.0 copy.14
  350.6 0.0 copy-done.2
  350.6 0.0 copy-done.3
  350.6 0.7 pad_maximum_fusion.2
  351.3 0.9 pad_maximum_fusion.1
  352.3 1.0 copy.15
  353.2 4.2 %copy.20 = bf16[1,2048,896]{2,1,0:T(8,128)(2,1)} copy(bf16[1,2048,896]{2,1,0:T(8,128)(2,1)} %bitcast.19) | data formatting | bytes 7340032
  (1 shorter events, 0.0 us)
Async XLA Ops:
  301.5 47.2 %copy-start.1 = (bf16[28,2304]{1,0:T(8,128)(2,1)S(1)}, bf16[28,2304]{1,0:T(8,128)(2,1)}, u32[]{:S(2)}) copy-start(bf16[28,2304]{1,0:T(8,128)(2,1)} %get-tuple-element.51) | copy-start | bytes 387076
  301.5 49.1 %copy-start.2 = (bf16[72,896]{1,0:T(8,128)(2,1)S(1)}, bf16[72,896]{1,0:T(8,128)(2,1)}, u32[]{:S(2)}) copy-start(bf16[72,896]{1,0:T(8,128)(2,1)} %get-tuple-element.55) | copy-start | bytes 387076
  301.5 49.1 %copy-start.3 = (bf16[72,896]{1,0:T(8,128)(2,1)S(1)}, bf16[72,896]{1,0:T(8,128)(2,1)}, u32[]{:S(2)}) copy-start(bf16[72,896]{1,0:T(8,128)(2,1)} %get-tuple-element.54) | copy-start | bytes 387076
  301.5 49.8 %copy-start = (bf16[28,2304]{1,0:T(8,128)(2,1)S(1)}, bf16[28,2304]{1,0:T(8,128)(2,1)}, u32[]{:S(2)}) copy-start(bf16[28,2304]{1,0:T(8,128)(2,1)} %get-tuple-element.53) | copy-start | bytes 387076
